TPU v7x, 32 devices: a whole 2x2x4 slice. The times are simulated.
32 devices in a mesh: dp: 2 (over x), tp: 16 (over y, z, core).
Axes of the slice: x: 2, y: 2, z: 4, core: 2. Of those that a mesh axis runs over, the one named last changes fastest.
Arguments:
- x: bfloat16 [4096, 8192], P('dp'), parts along dimension 0
- dy: bfloat16 [4096, 8192], P('dp'), parts along dimension 0
- gate: bfloat16 [4096, 28672], P('dp', 'tp'), parts along dimension 0
- up: bfloat16 [4096, 28672], P('dp', 'tp'), parts along dimension 0
- w_gate: bfloat16 [8192, 28672], P(None, 'tp')
- w_up: bfloat16 [8192, 28672], P(None, 'tp')
- w_down: bfloat16 [28672, 8192], P('tp')
Outputs:
- output 1: bfloat16 [4096, 8192], P('dp'), parts along dimension 0
- output 2: bfloat16 [16384, 28672], P('dp', 'tp'), parts along dimension 0
- output 3: bfloat16 [16384, 28672], P('dp', 'tp'), parts along dimension 0
- output 4: bfloat16 [57344, 8192], P(('dp', 'tp')), parts along dimension 0
There are 2 independent parts. A program takes and returns all parts, laid end to end along the dimension named above; an argument that names none is the same for every part.
All inputs are finite; a program needn't handle non-finite values.
Results may differ from a plain program's by a relative error of at most 0.012.
Values are sent between devices in bfloat16 or wider.
A program may use at most 2 GiB of HBM per device.

v0:
```python
import jax
import jax.numpy as jnp
from jax import lax
from jax.sharding import PartitionSpec as P


def act(gate, up):
    return jax.nn.silu(gate) * up


def solution(mesh):
    def step(x, dy, gate, up, w_gate, w_up, w_down):
        hidden, back = jax.vjp(act, gate.astype(jnp.float32), up.astype(jnp.float32))
        d_hidden = jnp.dot(dy, w_down.T, preferred_element_type=jnp.float32)
        d_gate, d_up = (g.astype(jnp.bfloat16) for g in back(d_hidden))
        term = jnp.dot(d_gate, w_gate.T, preferred_element_type=jnp.float32) + jnp.dot(d_up, w_up.T, preferred_element_type=jnp.float32)
        dx = lax.psum(term.astype(jnp.bfloat16), "tp")
        dw_gate = jnp.dot(x.T, d_gate, preferred_element_type=jnp.float32)
        dw_up = jnp.dot(x.T, d_up, preferred_element_type=jnp.float32)
        dw_down = jnp.dot(hidden.astype(jnp.bfloat16).T, dy, preferred_element_type=jnp.float32)
        return dx, *(g.astype(jnp.bfloat16) for g in (dw_gate, dw_up, dw_down))

    tokens, columns, rows = P("dp", None), P(None, "tp"), P("tp", None)
    return jax.shard_map(
        step,
        mesh=mesh,
        in_specs=(tokens, tokens, P("dp", "tp"), P("dp", "tp"), columns, columns, rows),
        out_specs=(tokens, P("dp", "tp"), P("dp", "tp"), P(("dp", "tp"), None)),
        check_vma=False,
    )
```

profile of v0, /device:TPU:0, one launch (start us, length us, event | category | flops | bytes accessed | tf_op | source)
XLA Modules:
  0.0 858.0 jit_solution(13898709635282472193)
XLA Ops:
  7.2 0.0 all-reduce.2.cloned.1.call-start
  7.2 81.3 %fusion.8 = (bf16[2048,1792]{1,0:T(8,128)(2,1)}, f32[2048,1792]{1,0:T(8,128)}) fusion(bf16[2048,1792]{1,0:T(8,128)(2,1)} %param.9, bf16[2048,1792]{1,0:T(8,128)(2,1)} %param.10, bf16[2048,8192]{1,0:T(8,128)(2,1)} %param.8, bf16[1792,8192]{1,0:T(8,128)(2,1)} %param.13), kind=kOutput, calls=%fused_computation.18 | convolution fusion | flops 60177252352 | bytes 99614720 | tf_op jit(solution)/shard_map/dot_general | solution.py:14
  88.5 70.6 %fusion.11 = f32[2048,8192]{1,0:T(8,128)} fusion(bf16[2048,1792]{1,0:T(8,128)(2,1)} %get-tuple-element.8, bf16[8192,1792]{1,0:T(8,128)(2,1)} %param.11), kind=kOutput, calls=%fused_computation.21 | convolution fusion | flops 60129542144 | bytes 103809024 | tf_op jit(solution)/shard_map/dot_general | solution.py:16
  159.1 101.4 %add_convert_fusion = bf16[2048,8192]{1,0:T(8,128)(2,1)} fusion(f32[2048,8192]{1,0:T(8,128)} %fusion.11, bf16[8192,1792]{1,0:T(8,128)(2,1)} %param.12, f32[2048,1792]{1,0:T(8,128)} %get-tuple-element.9, bf16[2048,1792]{1,0:T(8,128)(2,1)} %param.9), kind=kOutput, calls=%fused_computation | convolution fusion | flops 60188786688 | bytes 152043520 | tf_op jit(solution)/shard_map/dot_general | solution.py:16
  260.5 0.0 all-reduce.2.cloned.1.call-update
  260.5 84.0 %fusion.1 = bf16[8192,1792]{0,1:T(8,128)(2,1)} fusion(bf16[2048,8192]{1,0:T(8,128)(2,1)} %param.7, f32[2048,1792]{1,0:T(8,128)} %get-tuple-element.9, bf16[2048,1792]{1,0:T(8,128)(2,1)} %param.9), kind=kOutput, calls=%fused_computation.5 | convolution fusion | flops 60169912320 | bytes 84934656 | tf_op jit(solution)/shard_map/dot_general | solution.py:19
  344.5 69.2 %fusion = bf16[8192,1792]{0,1:T(8,128)(2,1)} fusion(bf16[2048,1792]{1,0:T(8,128)(2,1)} %get-tuple-element.8, bf16[2048,8192]{1,0:T(8,128)(2,1)} %param.7), kind=kOutput, calls=%fused_computation.4 | convolution fusion | flops 60144222208 | bytes 70254592 | tf_op jit(solution)/shard_map/dot_general | solution.py:18
  413.7 35.8 %copy.11 = bf16[8192,1792]{1,0:T(8,128)(2,1)} copy(bf16[8192,1792]{0,1:T(8,128)(2,1)} %fusion) | data formatting | bytes 58720256
  449.6 35.8 %copy.12 = bf16[8192,1792]{1,0:T(8,128)(2,1)} copy(bf16[8192,1792]{0,1:T(8,128)(2,1)} %fusion.1) | data formatting | bytes 58720256
  485.4 90.5 %convolution_convert_fusion = bf16[1792,8192]{1,0:T(8,128)(2,1)} fusion(bf16[2048,8192]{1,0:T(8,128)(2,1)} %param.8, bf16[2048,1792]{1,0:T(8,128)(2,1)} %param.10, bf16[2048,1792]{1,0:T(8,128)(2,1)} %param.9), kind=kOutput, calls=%fused_computation.1 | convolution fusion | flops 60173582336 | bytes 77594624 | tf_op jit(solution)/shard_map/dot_general | solution.py:20
  575.9 251.7 %all-reduce.2.cloned.1.call-done = bf16[2048,8192]{1,0:T(8,128)(2,1)} async-done(((bf16[2048,8192]{1,0:T(8,128)(2,1)}), bf16[2048,8192]{1,0:T(8,128)(2,1)}) %all-reduce.2.cloned.1.call-update) | async-done | bytes 33554448 | tf_op jit(solution)/shard_map/psum | solution.py:17
  827.6 23.0 %copy.14 = bf16[2048,8192]{1,0:T(8,128)(2,1)} copy(bf16[2048,8192]{1,0:T(8,128)(2,1)} %all-reduce.2.cloned.1.call-done) | data formatting | bytes 67108864
Async XLA Ops:
  7.2 820.5 %all-reduce.2.cloned.1.call-start = ((), (), s32[]{:S(2)}) async-start(), calls=%async_computation | async-start | bytes 67108864 | tf_op jit(solution)/shard_map/psum | solution.py:17
Sparse Core Ops, SparseCore 0:
  260.6 566.9 all-reduce.1
where the time goes:
time: 865 us; the launch traced here: 858 us
  matrix products  497 us (57%)
  waiting for transfers between devices  252 us (29%)
  local copies, waits for them, and re-layouts  94.7 us (11%)
  between operations  14.5 us (2%)
    psum x1, waiting for transfers between devices, step(): dx = lax.psum(term.astype(jnp.bfloat16), 'tp')  252 us
    dot_general x1, matrix products, step(): jnp.dot(d_up, w_up.T, preferred_element_type=jnp.float32)  101 us
    unnamed x3, local copies, waits for them, and re-layouts  94.7 us
    dot_general x1, matrix products, step(): jnp.dot(hidden.astype(jnp.bfloat16).T, dy, preferred_element_type=jnp.flo...  90.5 us
    dot_general x1, matrix products, step(): dw_up = jnp.dot(x.T, d_up, preferred_element_type=jnp.float32)  84 us
    dot_general x1, matrix products, step(): d_hidden = jnp.dot(dy, w_down.T, preferred_element_type=jnp.float32)  81.3 us
    dot_general x1, matrix products, step(): jnp.dot(d_gate, w_gate.T, preferred_element_type=jnp.float32)  70.6 us
    dot_general x1, matrix products, step(): dw_gate = jnp.dot(x.T, d_gate, preferred_element_type=jnp.float32)  69.2 us
  transfers between devices with their start and end apart: 1, of which 1 were waited for; matrix products, arithmetic and copies ran while one was open for 37% of the time, Pallas kernels for 0%

commit v1 on v0

v1 whole, which is shorter than its diff:
```python
import jax
import jax.numpy as jnp
from jax import lax
from jax.experimental import pallas as pl
from jax.experimental.pallas import tpu as pltpu
from jax.sharding import PartitionSpec as P

BF = jnp.bfloat16
F32 = jnp.float32
VMEM_LIMIT = 67043328
CHUNKS = 4
CHIPS = 8
TILES = 7
SLOTS = 10


def nt(a, b):
    return lax.dot_general(a, b, (((1,), (1,)), ((), ())), preferred_element_type=F32)


def tn(a, b):
    return lax.dot_general(a, b, (((0,), (0,)), ((), ())), preferred_element_type=F32)


def chip_at(q):
    return q + (q // 4) * (11 - 2 * q)


def reduce_kernel(
    dy, wd, gate, up, wg, wu,
    dgo, duo, hido, piece,
    dyb, wdb, gtb, utb, dg, du, hb, wgb, wub, own, precv, psend, rrecv, rsend,
    s_dy, s_wd, s_gt, s_ut, s_og, s_ou, s_pg, s_pu, s_h, s_dg, s_du, s_fin,
    s_psend, s_precv, s_rsend, s_rrecv, c_ring, c_part,
):
    M = dyb.shape[0]
    W = wgb.shape[1] // 2
    FT = wdb.shape[1]
    i = lax.axis_index("tp")
    core = i % 2
    chip = i // 2
    y = chip // 4
    z = chip % 4
    r = z + y * (7 - 2 * z)
    sgn = 1 - 2 * core
    nxt = {"tp": 2 * chip_at((r + sgn + 8) % 8) + core}
    prv = {"tp": 2 * chip_at((r - sgn + 8) % 8) + core}
    par = {"tp": 2 * chip + 1 - core}
    MESH = pl.DeviceIdType.MESH

    def rows_own(h):
        return pl.multiple_of((2 * chip_at((r - sgn * (1 + h) + 16) % 8) + core) * W, W)

    def rows_par(h):
        return pl.multiple_of((2 * chip_at((r + sgn * (1 + h) + 16) % 8) + 1 - core) * W, W)

    def ld(src, dst, sem):
        return pltpu.make_async_copy(src, dst, sem)

    def own_w(g):
        a, k = rows_own(g % 8), g % 2
        half = pl.ds(0, W)
        return [
            ld(wg.at[pl.ds(a, W), :], wgb.at[k, half], s_og.at[k]),
            ld(wu.at[pl.ds(a, W), :], wub.at[k, half], s_ou.at[k]),
        ]

    def par_w(g):
        a, k = rows_par(g % 8), (g + 1) % 2
        half = pl.ds(W, W)
        return [
            ld(wg.at[pl.ds(a, W), :], wgb.at[k, half], s_pg.at[k]),
            ld(wu.at[pl.ds(a, W), :], wub.at[k, half], s_pu.at[k]),
        ]

    def dh_in(k):
        c, j, b = k // TILES, k % TILES, k % 2
        rows, cols = pl.ds(pl.multiple_of(c * M, M), M), pl.ds(pl.multiple_of(j * FT, FT), FT)
        return [
            ld(wd.at[cols, :], wdb.at[b], s_wd.at[b]),
            ld(gate.at[rows, cols], gtb.at[b], s_gt.at[b]),
            ld(up.at[rows, cols], utb.at[b], s_ut.at[b]),
        ]

    def dy_in(c):
        return ld(dy.at[pl.ds(pl.multiple_of(c * M, M), M), :], dyb, s_dy)

    def dh_out(k):
        c, j, b = k // TILES, k % TILES, k % 2
        rows, cols = pl.ds(pl.multiple_of(c * M, M), M), pl.ds(pl.multiple_of(j * FT, FT), FT)
        return [
            ld(hb.at[b], hido.at[rows, cols], s_h.at[b]),
            ld(dg.at[c % 2, :, cols], dgo.at[rows, cols], s_dg.at[b]),
            ld(du.at[c % 2, :, cols], duo.at[rows, cols], s_du.at[b]),
        ]

    def fin(c):
        return ld(rsend.at[3], piece.at[pl.ds(pl.multiple_of(c * M, M), M), :], s_fin)

    def ring(m):
        return pltpu.make_async_remote_copy(
            rsend.at[m % 2], rrecv.at[m % 4], s_rsend.at[m % 2], s_rrecv.at[m % 4], device_id=nxt, device_id_type=MESH
        )

    def part(g):
        return pltpu.make_async_remote_copy(
            psend.at[g % 2], precv.at[g % 4], s_psend.at[g % 2], s_precv.at[g % 4], device_id=par, device_id_type=MESH
        )

    def start(copies):
        for c in copies:
            c.start()

    def wait(copies):
        for c in copies:
            c.wait()

    def dh_tile(k):
        c, j, b = k // TILES, k % TILES, k % 2
        cols = pl.ds(pl.multiple_of(j * FT, FT), FT)
        d = nt(dyb[...], wdb[b])
        g = gtb[b].astype(F32)
        u = utb[b].astype(F32)
        sig = 1.0 / (1.0 + jnp.exp(-g))
        silu = g * sig
        hb[b] = (silu * u).astype(BF)
        du[c % 2, :, cols] = (d * silu).astype(BF)
        dg[c % 2, :, cols] = (d * u * (sig * (1.0 + g * (1.0 - sig)))).astype(BF)

    def par_tile(g):
        k, b, half = (g // 8) % 2, (g + 1) % 2, pl.ds(W, W)
        psend[g % 2] = (nt(dg[k], wgb[b, half]) + nt(du[k], wub[b, half])).astype(BF)

    def own_tile(g):
        k, b, half = (g // 8) % 2, g % 2, pl.ds(0, W)
        own[g % SLOTS] = nt(dg[k], wgb[b, half]) + nt(du[k], wub[b, half])

    def both_tiles(g):
        k, b = (g // 8) % 2, g % 2
        term = nt(dg[k], wgb[b]) + nt(du[k], wub[b])
        own[g % SLOTS] = term[:, :W]
        psend[(g + 1) % 2] = term[:, W:].astype(BF)

    def dh_ready(k):
        wait(dh_in(k))

        @pl.when(k >= 2)
        def _():
            wait(dh_out(k - 2))

    def dh_done(k):
        start(dh_out(k))

        @pl.when(k + 2 < CHUNKS * TILES)
        def _():
            start(dh_in(k + 2))

    dy_in(0).start()
    start(dh_in(0))
    start(dh_in(1))
    start(par_w(0))
    start(own_w(0))
    start(par_w(1))
    start(own_w(1))
    barrier = pltpu.get_barrier_semaphore()
    for d in (nxt, prv, par):
        pl.semaphore_signal(barrier, inc=1, device_id=d, device_id_type=MESH)
    rrecv[4] = jnp.zeros((M, W), BF)
    dy_in(0).wait()

    @pl.loop(0, TILES)
    def _(k):
        dh_ready(k)
        dh_tile(k)
        dh_done(k)

    dy_in(1).start()
    pl.semaphore_wait(barrier, 3)
    wait(par_w(0))
    par_tile(0)
    part(0).start()
    start(par_w(2))

    STEPS = CHUNKS * 8
    SENDS = CHUNKS * 7

    def combine(g):
        own[g % SLOTS] = own[g % SLOTS] + precv[(g + 4) % 4].astype(F32)

    def credit():
        pl.semaphore_signal(c_ring, inc=1, device_id=prv, device_id_type=MESH)

    @pl.loop(0, STEPS)
    def _(t):
        c, s = t // 8, t % 8
        odd = t % 2
        first = 1 - (s + 6) // 7
        later = (c + 3) // 4
        m = (1 - later) * ((t + 7) // 2 - 4) + later * (7 * c - 4 + s)
        n = (1 - later) * ((t + 5) // 2 - 4) + later * (7 * c - 6 + s + first)
        adds = (odd == 1) | (t >= 10)
        takes = adds & (s != 1)
        sends = adds & (s != 0)
        ends = adds & (s == 0)
        has_dh = (s < 7) & (c < CHUNKS - 1)
        k = TILES * (c + 1) + s
        hop = odd * ((s - 1) // 2) + (1 - odd) * ((1 - first) * (3 + s // 2) + first * 7)
        tile = (8 * (c - (1 - odd) * (1 + first)) + hop + 2 * CHUNKS * SLOTS) % SLOTS
        on = 1 - (1 - odd) * ((41 - t) // 32)
        got = on * (1 - odd * ((8 - s) // 7))
        src = got * ((n + 8) % 4) + (1 - got) * 4
        dst = on * ((1 - first) * ((m + 8) % 2) + first * 3) + (1 - on) * 2

        wait(own_w(t))

        @pl.when(t + 1 < STEPS)
        def _():
            wait(par_w(t + 1))

        @pl.when((s == 0) & (c < CHUNKS - 1))
        def _():
            dy_in(c + 1).wait()

        @pl.when(has_dh)
        def _():
            dh_ready(k)

        @pl.when(t >= 1)
        def _():
            part(t - 1).wait_recv()
            part(t - 1).wait_send()

        @pl.when(takes)
        def _():
            ring(n).wait_recv()

        @pl.when(sends & (m >= 2))
        def _():
            ring(m - 2).wait_send()

        @pl.when(ends & (c >= 3))
        def _():
            fin(c - 3).wait()

        def add():
            combine(t - 1 + SLOTS * 4)
            rsend[dst] = (own[tile] + rrecv[src].astype(F32)).astype(BF)

        def send():
            @pl.when(sends & (m >= 4))
            def _():
                pl.semaphore_wait(c_ring, 1)

            @pl.when(sends)
            def _():
                ring(m).start()

            @pl.when(ends)
            def _():
                fin(c - 2).start()

            @pl.when(takes & (n < SENDS - 4))
            def _():
                credit()

        @pl.when(has_dh)
        def _():
            dh_tile(k)

            @pl.when(t >= 0)
            def _():
                both_tiles(t)

            add()
            send()
            dh_done(k)

        @pl.when(jnp.logical_not(has_dh))
        def _():
            add()
            send()
            own_tile(t)

            @pl.when(t + 1 < STEPS)
            def _():
                par_tile(t + 1)

        @pl.when(t + 1 < STEPS)
        def _():
            @pl.when(t >= 2)
            def _():
                pl.semaphore_wait(c_part, 1)

            part(t + 1).start()

        @pl.when(t < STEPS - 3)
        def _():
            pl.semaphore_signal(c_part, inc=1, device_id=par, device_id_type=MESH)

        @pl.when((s == 6) & (c < CHUNKS - 2))
        def _():
            dy_in(c + 2).start()

        @pl.when(t + 2 < STEPS)
        def _():
            start(own_w(t + 2))

        @pl.when(t + 3 < STEPS)
        def _():
            start(par_w(t + 3))

    part(STEPS - 1).wait_recv()
    part(STEPS - 1).wait_send()
    combine(STEPS - 1)
    n = SENDS - 5
    for tile in (STEPS - 9, STEPS - 4, STEPS - 3, STEPS - 2, STEPS - 1):
        ring(n).wait_recv()
        last = tile % 8 == 7
        if last:
            fin(0).wait()
            dst = 3
        else:
            m = n + 1
            ring(m - 2).wait_send()
            dst = m % 2
        rsend[dst] = (own[tile % SLOTS] + rrecv[n % 4].astype(F32)).astype(BF)
        if last:
            fin(tile // 8).start()
        else:
            pl.semaphore_wait(c_ring, 1)
            ring(m).start()
        if n < SENDS - 4:
            credit()
        n += 1
    ring(SENDS - 2).wait_send()
    ring(SENDS - 1).wait_send()
    fin(0).wait()
    wait(dh_out(CHUNKS * TILES - 2))
    wait(dh_out(CHUNKS * TILES - 1))


def reduce_call(dy, wd, gate, up, wg, wu):
    T, D = dy.shape
    F = gate.shape[1]
    M, W, FT = T // CHUNKS, D // (2 * CHIPS), F // TILES
    hbm = pl.BlockSpec(memory_space=pltpu.HBM)
    dma, reg = pltpu.SemaphoreType.DMA, pltpu.SemaphoreType.REGULAR
    v = pltpu.VMEM
    return pl.pallas_call(
        reduce_kernel,
        in_specs=[hbm] * 6,
        out_specs=[hbm] * 4,
        out_shape=[jax.ShapeDtypeStruct((T, F), BF)] * 3 + [jax.ShapeDtypeStruct((T, W), BF)],
        scratch_shapes=[
            v((M, D), BF), v((2, FT, D), BF), v((2, M, FT), BF), v((2, M, FT), BF),
            v((2, M, F), BF), v((2, M, F), BF), v((2, M, FT), BF),
            v((2, 2 * W, F), BF), v((2, 2 * W, F), BF),
            v((SLOTS, M, W), F32), v((4, M, W), BF), v((2, M, W), BF), v((5, M, W), BF), v((4, M, W), BF),
            dma(()), *[dma((2,))] * 10, dma(()),
            dma((2,)), dma((4,)), dma((2,)), dma((4,)), reg, reg,
        ],
        compiler_params=pltpu.CompilerParams(collective_id=0, has_side_effects=True, vmem_limit_bytes=VMEM_LIMIT),
        name="dx_reduce",
    )(dy, wd, gate, up, wg, wu)


def gate_up_grads(x, dg, du, bm):
    T, D = x.shape
    F = dg.shape[1]

    def body(x_ref, dg_ref, du_ref, og, ou):
        og[...] = tn(x_ref[...], dg_ref[...]).astype(BF)
        ou[...] = tn(x_ref[...], du_ref[...]).astype(BF)

    one = pl.BlockSpec((T, F), lambda i: (0, 0), pipeline_mode=pl.Buffered(1))
    return pl.pallas_call(
        body,
        grid=(D // bm,),
        in_specs=[pl.BlockSpec((T, bm), lambda i: (0, i)), one, one],
        out_specs=[pl.BlockSpec((bm, F), lambda i: (i, 0))] * 2,
        out_shape=[jax.ShapeDtypeStruct((D, F), BF)] * 2,
        compiler_params=pltpu.CompilerParams(vmem_limit_bytes=VMEM_LIMIT),
        cost_estimate=pl.CostEstimate(flops=4 * T * D * F, bytes_accessed=2 * (T * D + 2 * T * F + 2 * D * F), transcendentals=0),
        name="dw_gate_up",
    )(x, dg, du)


def down_grad(hid, dy, bn, lo, hi, moved=(), prev=()):
    T, D = dy.shape
    F = hid.shape[1]
    steps = hi - lo
    mb = T // steps

    def body(h_ref, dy_ref, *refs):
        if moved:
            refs[-1][...] = refs[0][...]
        o_ref = refs[-2] if moved else refs[-1]
        o_ref[...] = tn(h_ref[...], dy_ref[...]).astype(BF)

    rows = [pl.BlockSpec((mb, D), lambda i: (i, 0))] if moved else []
    return pl.pallas_call(
        body,
        grid=(steps,),
        in_specs=[
            pl.BlockSpec((T, F), lambda i: (0, 0), pipeline_mode=pl.Buffered(1)),
            pl.BlockSpec((T, bn), lambda i: (0, lo + i)),
            *rows,
            *[pl.BlockSpec(memory_space=pl.ANY)] * len(prev),
        ],
        out_specs=[pl.BlockSpec((F, bn), lambda i: (0, lo + i)), *rows],
        out_shape=[jax.ShapeDtypeStruct((F, D), BF), *[jax.ShapeDtypeStruct((T, D), BF)] * len(moved)],
        input_output_aliases={2 + len(moved): 0} if prev else {},
        compiler_params=pltpu.CompilerParams(vmem_limit_bytes=VMEM_LIMIT),
        cost_estimate=pl.CostEstimate(
            flops=2 * T * F * bn * steps,
            bytes_accessed=2 * (T * F + (T + F) * bn * steps + 2 * T * D * len(moved)),
            transcendentals=0,
        ),
        name="dw_down",
    )(hid, dy, *moved, *prev)


def solution(mesh):
    def step(x, dy, gate, up, w_gate, w_up, w_down):
        D = x.shape[1]
        dg, du, hid, piece = reduce_call(dy, w_down, gate, up, w_gate, w_up)
        gathered = lax.all_gather(piece, "tp", axis=1, tiled=True)
        dw_gate, dw_up = gate_up_grads(x, dg, du, D // 16)
        bn = D // 16
        first = down_grad(hid, dy, bn, 0, 8)
        dw_down, dx = down_grad(hid, dy, bn, 8, 16, (gathered,), first)
        return dx, dw_gate, dw_up, dw_down

    tokens, columns, rows = P("dp", None), P(None, "tp"), P("tp", None)
    return jax.shard_map(
        step,
        mesh=mesh,
        in_specs=(tokens, tokens, P("dp", "tp"), P("dp", "tp"), columns, columns, rows),
        out_specs=(tokens, P("dp", "tp"), P("dp", "tp"), P(("dp", "tp"), None)),
        check_vma=False,
    )
```

time: 865 us -> 509 us (0.59)
  matrix products: 497 us -> 0 us
  Pallas kernels: 0 us -> 494 us
  waiting for transfers between devices: 252 us -> 0.02 us
  local copies, waits for them, and re-layouts: 94.7 us -> 0 us
    dot_general x6 -> x0, matrix products: 497 us -> none  [the longest x1 101 us: step(): jnp.dot(d_up, w_up.T, preferred_element_type=jnp.float32)]
    pallas_call x0 -> x4, Pallas kernels: none -> 494 us  [the longest x1 282 us: reduce_call(): pl.pallas_call(reduce_kernel, in_specs=[hbm] * 6, out_specs=[hbm] * 4, ou...]
    psum x1 -> x0, waiting for transfers between devices: 252 us -> none  [step(): dx = lax.psum(term.astype(jnp.bfloat16), 'tp')]
    unnamed x3 -> x0, local copies, waits for them, and re-layouts: 94.7 us -> none
  transfers between devices with their start and end apart: 1 -> 1, of which waited for: 1 -> 0; matrix products, arithmetic and copies ran while one was open for 37% -> 0% of each run, Pallas kernels for 0% -> 33%
where the time goes in v1:
time: 509 us; the launch traced here: 508 us
  Pallas kernels  494 us (97%)
  between operations  14 us (3%)
    pallas_call x1, Pallas kernels, reduce_call(): pl.pallas_call(reduce_kernel, in_specs=[hbm] * 6, out_specs=[hbm] * 4, ou...  282 us
    pallas_call x1, Pallas kernels, gate_up_grads(): pl.pallas_call(body, grid=(D // bm,), in_specs=[pl.BlockSpec((T, bm), lam...  132 us
    pallas_call x2, Pallas kernels, down_grad(): pl.pallas_call(body, grid=(steps,), in_specs=[pl.BlockSpec((T, F), lambda...  80.7 us
  transfers between devices with their start and end apart: 1, of which 0 were waited for; matrix products, arithmetic and copies ran while one was open for 0% of the time, Pallas kernels for 33%

profile of v1, /device:TPU:0, one launch (start us, length us, event | category | flops | bytes accessed | tf_op | source)
XLA Modules:
  0.0 508.5 jit_solution(6148917610257012686)
XLA Ops:
  7.2 0.0 all-gather.2.cloned.1.call-start
  7.2 282.0 %dx_reduce.1 = (bf16[2048,1792]{1,0:T(8,128)(2,1)}, bf16[2048,1792]{1,0:T(8,128)(2,1)}, bf16[2048,1792]{1,0:T(8,128)(2,1)}, bf16[2048,512]{1,0:T(8,128)(2,1)}) custom-call(bf16[2048,8192]{1,0:T(8,128)(2,1)} %dy_ref.3, bf16[1792,8192]{1,0:T(8,128)(2,1)} %wd.1, bf16[2048,1792]{1,0:T(8,128)(2,1)} %gate.1, bf16[2048,1792]{1,0:T(8,128)(2,1)} %up.1, ...), custom_call_target="tpu_custom_call" | custom-call | tf_op jit(solution)/shard_map/dx_reduce/pallas_call | solution.py:349
  289.2 0.0 all-gather.2.cloned.1.call-update
  289.3 37.3 %dw_down.2.refs_1_ = bf16[1792,8192]{1,0:T(8,128)(2,1)} custom-call(bf16[2048,1792]{1,0:T(8,128)(2,1)} %get-tuple-element.12.h_ref, bf16[2048,8192]{1,0:T(8,128)(2,1)} %dy_ref.3), custom_call_target="tpu_custom_call" | custom-call | flops 30064771072 | bytes 38797312 | tf_op jit(solution)/shard_map/dw_down/pallas_call | solution.py:401
  326.6 131.7 %dw_gate_up.1 = (bf16[8192,1792]{1,0:T(8,128)(2,1)}, bf16[8192,1792]{1,0:T(8,128)(2,1)}) custom-call(bf16[2048,8192]{1,0:T(8,128)(2,1)} %x_ref.1, bf16[2048,1792]{1,0:T(8,128)(2,1)} %get-tuple-element.15.dg_ref, bf16[2048,1792]{1,0:T(8,128)(2,1)} %get-tuple-element.16.du_ref), custom_call_target="tpu_custom_call" | custom-call | flops 120259084288 | bytes 106954752 | tf_op jit(solution)/shard_map/dw_gate_up/pallas_call | solution.py:376
  458.2 0.0 all-gather.2.cloned.1.call-done.refs_0_
  458.2 43.4 %dw_down.3 = (bf16[1792,8192]{1,0:T(8,128)(2,1)}, bf16[2048,8192]{1,0:T(8,128)(2,1)}) custom-call(bf16[2048,1792]{1,0:T(8,128)(2,1)} %get-tuple-element.12.h_ref, bf16[2048,8192]{1,0:T(8,128)(2,1)} %dy_ref.3, bf16[2048,8192]{1,0:T(8,128)(2,1)} %all-gather.2.cloned.1.call-done.refs_0_, bf16[1792,8192]{1,0:T(8,128)(2,1)} %dw_down.2.refs_1_), custom_call_target="tpu_custom_call", output_to_operand_aliasing={{0}: (3, {})} | custom-call | flops 30064771072 | bytes 105906176 | tf_op jit(solution)/shard_map/dw_down/pallas_call | solution.py:401
Async XLA Ops:
  7.2 451.1 %all-gather.2.cloned.1.call-start = ((), (), s32[]{:S(2)}) async-start(), calls=%async_computation | async-start | bytes 35651584 | tf_op jit(solution)/shard_map/all_gather | solution.py:427
Sparse Core Ops, SparseCore 0:
  289.4 165.1 all-gather.1

commit v2 on v1

v2 whole, which is shorter than its diff:
```python
import jax
import jax.numpy as jnp
from jax import lax
from jax.experimental import pallas as pl
from jax.experimental.pallas import tpu as pltpu
from jax.sharding import PartitionSpec as P

BF = jnp.bfloat16
F32 = jnp.float32
VMEM_LIMIT = 67043328
CHUNKS = 4
CHIPS = 8
TILES = 7
STEPS = CHUNKS * CHIPS
SENDS = CHUNKS * (CHIPS - 1)


def nt(a, b):
    return lax.dot_general(a, b, (((1,), (1,)), ((), ())), preferred_element_type=F32)


def tn(a, b):
    return lax.dot_general(a, b, (((0,), (0,)), ((), ())), preferred_element_type=F32)


def chip_at(q):
    return q + (q // 4) * (11 - 2 * q)


def reduce_kernel(
    dy, wd, gate, up, wg, wu,
    dguo, hido, piece,
    dyb, wdb, gtb, utb, dg, du, dgn, dun, hb, wgb, wub, own, precv, psend, rrecv, rsend,
    s_dy, s_wd, s_gt, s_ut, s_og, s_ou, s_pg, s_pu, s_h, s_dg, s_du, s_fin,
    s_psend, s_precv, s_rsend, s_rrecv, c_ring, c_part,
):
    M, D = dyb.shape[1:]
    W = wgb.shape[1] // 2
    F, FT = dg.shape[1], wdb.shape[1]
    H = M // 2
    i = lax.axis_index("tp")
    core = i % 2
    chip = i // 2
    y = chip // 4
    z = chip % 4
    r = z + y * (7 - 2 * z)
    sgn = 1 - 2 * core
    nxt = {"tp": 2 * chip_at((r + sgn + 8) % 8) + core}
    prv = {"tp": 2 * chip_at((r - sgn + 8) % 8) + core}
    par = {"tp": 2 * chip + 1 - core}
    MESH = pl.DeviceIdType.MESH

    def rows_own(h):
        return pl.multiple_of((2 * chip_at((r - sgn * (1 + h) + 16) % 8) + core) * W, W)

    def rows_par(h):
        return pl.multiple_of((2 * chip_at((r + sgn * (1 + h) + 16) % 8) + 1 - core) * W, W)

    ld = pltpu.make_async_copy

    def own_w(g):
        a, k, half = rows_own(g % 8), g % 2, pl.ds(0, W)
        return [
            ld(wg.at[pl.ds(a, W), :], wgb.at[k, half], s_og.at[k]),
            ld(wu.at[pl.ds(a, W), :], wub.at[k, half], s_ou.at[k]),
        ]

    def par_w(g):
        a, k, half = rows_par(g % 8), (g + 1) % 2, pl.ds(W, W)
        return [
            ld(wg.at[pl.ds(a, W), :], wgb.at[k, half], s_pg.at[k]),
            ld(wu.at[pl.ds(a, W), :], wub.at[k, half], s_pu.at[k]),
        ]

    def dh_place(k):
        c, j = k // TILES, k % TILES
        return pl.ds(pl.multiple_of(c * M, M), M), pl.ds(pl.multiple_of(j * FT, FT), FT)

    def dh_in(k):
        b = k % 2
        rows, cols = dh_place(k)
        return [
            ld(wd.at[cols, :], wdb.at[b], s_wd.at[b]),
            ld(gate.at[rows, cols], gtb.at[b], s_gt.at[b]),
            ld(up.at[rows, cols], utb.at[b], s_ut.at[b]),
        ]

    def dy_in(c, p):
        n = M // 4
        return ld(dy.at[pl.ds(pl.multiple_of(c * M + p * n, n), n), :], dyb.at[c % 2, pl.ds(p * n, n)], s_dy.at[p])

    def dh_out(k, dg, du):
        b = k % 2
        rows, cols = dh_place(k)
        return [
            ld(hb.at[b], hido.at[rows, cols], s_h.at[b]),
            ld(dg.at[:, cols], dguo.at[rows, cols], s_dg.at[b]),
            ld(du.at[:, cols], dguo.at[rows, pl.ds(pl.multiple_of(F + k % TILES * FT, FT), FT)], s_du.at[b]),
        ]

    def fin(e, c):
        return ld(rsend.at[e, 2], piece.at[pl.ds(pl.multiple_of(c * M + e * H, H), H), :], s_fin.at[e])

    def ring(e, m):
        return pltpu.make_async_remote_copy(
            rsend.at[e, m % 2], rrecv.at[e, m % 3], s_rsend.at[e, m % 2], s_rrecv.at[e, m % 3], device_id=nxt, device_id_type=MESH
        )

    def part(g):
        return pltpu.make_async_remote_copy(
            psend.at[g % 2], precv.at[g % 4], s_psend.at[g % 2], s_precv.at[g % 4], device_id=par, device_id_type=MESH
        )

    def start(copies):
        for c in copies:
            c.start()

    def wait(copies):
        for c in copies:
            c.wait()

    def dh_tile(k, dg, du):
        b, cols = k % 2, dh_place(k)[1]
        d = nt(dyb[(k // TILES) % 2], wdb[b])
        g = gtb[b].astype(F32)
        u = utb[b].astype(F32)
        sig = lax.logistic(g)
        silu = g * sig
        hb[b] = (silu * u).astype(BF)
        du[:, cols] = (d * silu).astype(BF)
        dg[:, cols] = (d * u * (sig * (1.0 + g * (1.0 - sig)))).astype(BF)

    def own_tile(g):
        b, half = g % 2, pl.ds(0, W)
        own[g % 2] = nt(dg[...], wgb[b, half]) + nt(du[...], wub[b, half])

    def par_tile(g, dg, du):
        b, half = (g + 1) % 2, pl.ds(W, W)
        psend[g % 2] = (nt(dg[...], wgb[b, half]) + nt(du[...], wub[b, half])).astype(BF)

    def add(e, g, src, dst):
        rows = pl.ds(e * H, H)
        total = own[g % 2, rows] + precv[(g + 4) % 4, rows].astype(F32) + rrecv[e, src].astype(F32)
        rsend[e, dst] = total.astype(BF)

    def dh_ready(k):
        wait(dh_in(k))

        @pl.when(k >= 2)
        def _():
            wait(dh_out(k - 2, dg, du))

    def dh_done(k, dg, du):
        start(dh_out(k, dg, du))

        @pl.when(k + 2 < CHUNKS * TILES)
        def _():
            start(dh_in(k + 2))

    start(dh_in(0))
    for p in range(4):
        dy_in(0, p).start()
    start(dh_in(1))
    start(par_w(0))
    start(own_w(0))
    start(par_w(1))
    start(own_w(1))
    barrier = pltpu.get_barrier_semaphore()
    for d in (nxt, prv, par):
        pl.semaphore_signal(barrier, inc=1, device_id=d, device_id_type=MESH)
    for e in range(2):
        rrecv[e, 3] = jnp.zeros((H, W), BF)

    @pl.loop(0, TILES)
    def _(k):
        @pl.when(k == 0)
        def _():
            for p in range(4):
                dy_in(0, p).wait()

        dh_ready(k)
        dh_tile(k, dg, du)
        dh_done(k, dg, du)

        @pl.when(k < 4)
        def _():
            dy_in(1, k).start()

    wait(par_w(0))
    par_tile(0, dg, du)
    pl.semaphore_wait(barrier, 3)
    part(0).start()
    start(par_w(2))

    @pl.loop(0, STEPS)
    def _(t):
        c, s = t // 8, t % 8
        has_dh = (s < 7) & (c < CHUNKS - 1)
        k = TILES * (c + 1) + s
        g = t - 1
        h = (g + 8) % 8
        m = 7 * ((g + 8) // 8 - 1) + h
        adds = t >= 1
        takes = adds & (h >= 1)
        sends = adds & (h <= 6)
        ends = adds & (h == 7)
        last = (h + 1) // 8
        got = (h + 7) // 8 * (1 - (STEPS - t) // STEPS)
        src = got * ((m + 2) % 3) + (1 - got) * 3
        dst = (1 - last) * (m % 2) + last * 2

        wait(own_w(t))

        @pl.when(t + 1 < STEPS)
        def _():
            wait(par_w(t + 1))

        @pl.when((s == 0) & (c < CHUNKS - 1))
        def _():
            for p in range(4):
                dy_in(c + 1, p).wait()

        @pl.when(has_dh)
        def _():
            dh_ready(k)

        @pl.when(adds)
        def _():
            part(g).wait_recv()
            part(g).wait_send()

        @pl.when(sends & (m >= 2))
        def _():
            for e in range(2):
                ring(e, m - 2).wait_send()

        @pl.when(sends & (m >= 3))
        def _():
            for e in range(2):
                pl.semaphore_wait(c_ring.at[e], 1)

        @pl.when(ends & (t >= 16))
        def _():
            for e in range(2):
                fin(e, c - 2).wait()

        def pass_on(e):
            @pl.when(takes)
            def _():
                ring(e, m - 1).wait_recv()

            add(e, g, src, dst)

            @pl.when(sends)
            def _():
                ring(e, m).start()

        pass_on(0)

        @pl.when(has_dh)
        def _():
            dh_tile(k, dgn, dun)

        @pl.when(jnp.logical_not(has_dh))
        def _():
            own_tile(t)

        pass_on(1)

        @pl.when(has_dh)
        def _():
            own_tile(t)
            par_tile(t + 1, dg, du)
            dh_done(k, dgn, dun)

        @pl.when((s < 7) & (c == CHUNKS - 1))
        def _():
            par_tile(t + 1, dg, du)

        @pl.when((s == 7) & (c < CHUNKS - 1))
        def _():
            par_tile(t + 1, dgn, dun)
            dg[...] = dgn[...]
            du[...] = dun[...]

        @pl.when(ends)
        def _():
            for e in range(2):
                fin(e, c - 1).start()

        @pl.when(t + 1 < STEPS)
        def _():
            @pl.when(t >= 2)
            def _():
                pl.semaphore_wait(c_part, 1)

            part(t + 1).start()

        @pl.when(takes & (m - 1 < SENDS - 3))
        def _():
            for e in range(2):
                pl.semaphore_signal(c_ring.at[e], inc=1, device_id=prv, device_id_type=MESH)

        @pl.when(t < STEPS - 3)
        def _():
            pl.semaphore_signal(c_part, inc=1, device_id=par, device_id_type=MESH)

        @pl.when((s < 4) & (c < CHUNKS - 2))
        def _():
            dy_in(c + 2, s).start()

        @pl.when(t + 2 < STEPS)
        def _():
            start(own_w(t + 2))

        @pl.when(t + 3 < STEPS)
        def _():
            start(par_w(t + 3))

    part(STEPS - 1).wait_recv()
    part(STEPS - 1).wait_send()
    for e in range(2):
        fin(e, CHUNKS - 2).wait()
        ring(e, SENDS - 1).wait_recv()
        add(e, STEPS - 1, (SENDS - 1) % 3, 2)
        fin(e, CHUNKS - 1).start()
    for e in range(2):
        ring(e, SENDS - 2).wait_send()
        ring(e, SENDS - 1).wait_send()
        fin(e, CHUNKS - 1).wait()
    wait(dh_out(CHUNKS * TILES - 2, dgn, dun))
    wait(dh_out(CHUNKS * TILES - 1, dgn, dun))


def reduce_call(dy, wd, gate, up, wg, wu):
    T, D = dy.shape
    F = gate.shape[1]
    M, W, FT = T // CHUNKS, D // (2 * CHIPS), F // TILES
    hbm = pl.BlockSpec(memory_space=pltpu.HBM)
    dma, reg = pltpu.SemaphoreType.DMA, pltpu.SemaphoreType.REGULAR
    v = pltpu.VMEM
    return pl.pallas_call(
        reduce_kernel,
        in_specs=[hbm] * 6,
        out_specs=[hbm] * 3,
        out_shape=[jax.ShapeDtypeStruct((T, n), BF) for n in (2 * F, F, W)],
        scratch_shapes=[
            v((2, M, D), BF), v((2, FT, D), BF), v((2, M, FT), BF), v((2, M, FT), BF),
            v((M, F), BF), v((M, F), BF), v((M, F), BF), v((M, F), BF), v((2, M, FT), BF), v((2, 2 * W, F), BF), v((2, 2 * W, F), BF),
            v((2, M, W), F32), v((4, M, W), BF), v((2, M, W), BF), v((2, 4, M // 2, W), BF), v((2, 3, M // 2, W), BF),
            dma((4,)), *[dma((2,))] * 11,
            dma((2,)), dma((4,)), dma((2, 2)), dma((2, 3)), reg((2,)), reg,
        ],
        compiler_params=pltpu.CompilerParams(collective_id=0, has_side_effects=True, vmem_limit_bytes=VMEM_LIMIT),
        name="dx_reduce",
    )(dy, wd, gate, up, wg, wu)


def gate_up_grads(x, dgu, bm):
    T, D = x.shape
    F = dgu.shape[1] // 2

    def body(x_ref, d_ref, og, ou):
        both = tn(x_ref[...], d_ref[...])
        og[...] = both[:, :F].astype(BF)
        ou[...] = both[:, F:].astype(BF)

    return pl.pallas_call(
        body,
        grid=(D // bm,),
        in_specs=[
            pl.BlockSpec((T, bm), lambda i: (0, i)),
            pl.BlockSpec((T, 2 * F), lambda i: (0, 0), pipeline_mode=pl.Buffered(1)),
        ],
        out_specs=[pl.BlockSpec((bm, F), lambda i: (i, 0))] * 2,
        out_shape=[jax.ShapeDtypeStruct((D, F), BF)] * 2,
        compiler_params=pltpu.CompilerParams(vmem_limit_bytes=VMEM_LIMIT),
        cost_estimate=pl.CostEstimate(flops=4 * T * D * F, bytes_accessed=2 * (T * D + 2 * T * F + 2 * D * F), transcendentals=0),
        name="dw_gate_up",
    )(x, dgu)


def down_grad(hid, dy, bn, lo, hi, moved=(), prev=()):
    T, D = dy.shape
    F = hid.shape[1]
    steps = hi - lo
    mb = T // steps

    def body(h_ref, dy_ref, *refs):
        if moved:
            refs[-1][...] = refs[0][...]
        o_ref = refs[-2] if moved else refs[-1]
        o_ref[...] = tn(h_ref[...], dy_ref[...]).astype(BF)

    rows = [pl.BlockSpec((mb, D), lambda i: (i, 0))] if moved else []
    return pl.pallas_call(
        body,
        grid=(steps,),
        in_specs=[
            pl.BlockSpec((T, F), lambda i: (0, 0), pipeline_mode=pl.Buffered(1)),
            pl.BlockSpec((T, bn), lambda i: (0, lo + i)),
            *rows,
            *[pl.BlockSpec(memory_space=pl.ANY)] * len(prev),
        ],
        out_specs=[pl.BlockSpec((F, bn), lambda i: (0, lo + i)), *rows],
        out_shape=[jax.ShapeDtypeStruct((F, D), BF), *[jax.ShapeDtypeStruct((T, D), BF)] * len(moved)],
        input_output_aliases={2 + len(moved): 0} if prev else {},
        compiler_params=pltpu.CompilerParams(vmem_limit_bytes=VMEM_LIMIT),
        cost_estimate=pl.CostEstimate(
            flops=2 * T * F * bn * steps,
            bytes_accessed=2 * (T * F + (T + F) * bn * steps + 2 * T * D * len(moved)),
            transcendentals=0,
        ),
        name="dw_down",
    )(hid, dy, *moved, *prev)


def solution(mesh):
    def step(x, dy, gate, up, w_gate, w_up, w_down):
        D = x.shape[1]
        dgu, hid, piece = reduce_call(dy, w_down, gate, up, w_gate, w_up)
        gathered = lax.all_gather(piece, "tp", axis=1, tiled=True)
        dw_gate, dw_up = gate_up_grads(x, dgu, D // 16)
        bn = D // 16
        first = down_grad(hid, dy, bn, 0, 8)
        dw_down, dx = down_grad(hid, dy, bn, 8, 16, (gathered,), first)
        return dx, dw_gate, dw_up, dw_down

    tokens, columns, rows = P("dp", None), P(None, "tp"), P("tp", None)
    return jax.shard_map(
        step,
        mesh=mesh,
        in_specs=(tokens, tokens, P("dp", "tp"), P("dp", "tp"), columns, columns, rows),
        out_specs=(tokens, P("dp", "tp"), P("dp", "tp"), P(("dp", "tp"), None)),
        check_vma=False,
    )
```

time: 509 us -> 465 us (0.914)
  Pallas kernels: 494 us -> 451 us
    pallas_call x1, Pallas kernels: 282 us -> 239 us  [reduce_call(): pl.pallas_call(reduce_kernel, in_specs=[hbm] * 6, out_specs=[hbm] * 3, ou...]
  transfers between devices with their start and end apart: 1 -> 1, of which waited for: 0 -> 0; matrix products, arithmetic and copies ran while one was open for 0% -> 0% of each run, Pallas kernels for 33% -> 36%
where the time goes in v2:
time: 465 us
  Pallas kernels  451 us (97%)
  between operations  14 us (3%)
    pallas_call x1, Pallas kernels, reduce_call(): pl.pallas_call(reduce_kernel, in_specs=[hbm] * 6, out_specs=[hbm] * 3, ou...  239 us
    pallas_call x1, Pallas kernels, gate_up_grads(): pl.pallas_call(body, grid=(D // bm,), in_specs=[pl.BlockSpec((T, bm), lam...  132 us
    pallas_call x2, Pallas kernels, down_grad(): pl.pallas_call(body, grid=(steps,), in_specs=[pl.BlockSpec((T, F), lambda...  80.7 us
  transfers between devices with their start and end apart: 1, of which 0 were waited for; matrix products, arithmetic and copies ran while one was open for 0% of the time, Pallas kernels for 36%

profile of v2, /device:TPU:0, one launch (start us, length us, event | category | flops | bytes accessed | tf_op | source)
XLA Modules:
  0.0 465.0 jit_solution(11103825373562437143)
XLA Ops:
  7.2 0.0 all-gather.2.cloned.1.call-start
  7.2 238.6 %dx_reduce.1 = (bf16[2048,3584]{1,0:T(8,128)(2,1)}, bf16[2048,1792]{1,0:T(8,128)(2,1)}, bf16[2048,512]{1,0:T(8,128)(2,1)}) custom-call(bf16[2048,8192]{1,0:T(8,128)(2,1)} %dy_ref.3, bf16[1792,8192]{1,0:T(8,128)(2,1)} %wd.1, bf16[2048,1792]{1,0:T(8,128)(2,1)} %gate.1, bf16[2048,1792]{1,0:T(8,128)(2,1)} %up.1, bf16[8192,1792]{1,0:T(8,128)(2,1)} %wg.1, ...), custom_call_target="tpu_custom_call" | custom-call | tf_op jit(solution)/shard_map/dx_reduce/pallas_call | solution.py:342
  245.8 0.0 all-gather.2.cloned.1.call-update
  245.9 37.3 %dw_down.2.refs_1_ = bf16[1792,8192]{1,0:T(8,128)(2,1)} custom-call(bf16[2048,1792]{1,0:T(8,128)(2,1)} %get-tuple-element.11.h_ref, bf16[2048,8192]{1,0:T(8,128)(2,1)} %dy_ref.3), custom_call_target="tpu_custom_call" | custom-call | flops 30064771072 | bytes 38797312 | tf_op jit(solution)/shard_map/dw_down/pallas_call | solution.py:396
  283.2 131.5 %dw_gate_up.1 = (bf16[8192,1792]{1,0:T(8,128)(2,1)}, bf16[8192,1792]{1,0:T(8,128)(2,1)}) custom-call(bf16[2048,8192]{1,0:T(8,128)(2,1)} %x_ref.1, bf16[2048,3584]{1,0:T(8,128)(2,1)} %get-tuple-element.14.d_ref), custom_call_target="tpu_custom_call" | custom-call | flops 120259084288 | bytes 106954752 | tf_op jit(solution)/shard_map/dw_gate_up/pallas_call | solution.py:368
  414.7 0.0 all-gather.2.cloned.1.call-done.refs_0_
  414.7 43.4 %dw_down.3 = (bf16[1792,8192]{1,0:T(8,128)(2,1)}, bf16[2048,8192]{1,0:T(8,128)(2,1)}) custom-call(bf16[2048,1792]{1,0:T(8,128)(2,1)} %get-tuple-element.11.h_ref, bf16[2048,8192]{1,0:T(8,128)(2,1)} %dy_ref.3, bf16[2048,8192]{1,0:T(8,128)(2,1)} %all-gather.2.cloned.1.call-done.refs_0_, bf16[1792,8192]{1,0:T(8,128)(2,1)} %dw_down.2.refs_1_), custom_call_target="tpu_custom_call", output_to_operand_aliasing={{0}: (3, {})} | custom-call | flops 30064771072 | bytes 105906176 | tf_op jit(solution)/shard_map/dw_down/pallas_call | solution.py:396
Async XLA Ops:
  7.2 407.6 %all-gather.2.cloned.1.call-start = ((), (), s32[]{:S(2)}) async-start(), calls=%async_computation | async-start | bytes 35651584 | tf_op jit(solution)/shard_map/all_gather | solution.py:422
Sparse Core Ops, SparseCore 0:
  246.0 166.2 all-gather.1

commit v3 on v2

--- a/solution.py
+++ b/solution.py
@@ -13,6 +13,7 @@
 TILES = 7
 STEPS = CHUNKS * CHIPS
 SENDS = CHUNKS * (CHIPS - 1)
+EXTRA = 8
 
 
 def nt(a, b):
@@ -29,9 +30,9 @@
 
 def reduce_kernel(
     dy, wd, gate, up, wg, wu,
-    dguo, hido, piece,
-    dyb, wdb, gtb, utb, dg, du, dgn, dun, hb, wgb, wub, own, precv, psend, rrecv, rsend,
-    s_dy, s_wd, s_gt, s_ut, s_og, s_ou, s_pg, s_pu, s_h, s_dg, s_du, s_fin,
+    dguo, hido, piece, extra,
+    dyb, wdb, gtb, utb, dg, du, dgn, dun, hb, wgb, wub, own, precv, psend, rrecv, rsend, fout,
+    s_dy, s_fd, s_fo, s_wd, s_gt, s_ut, s_og, s_ou, s_pg, s_pu, s_h, s_dg, s_du, s_fin,
     s_psend, s_precv, s_rsend, s_rrecv, c_ring, c_part,
 ):
     M, D = dyb.shape[1:]
@@ -98,6 +99,17 @@
             ld(du.at[:, cols], dguo.at[rows, pl.ds(pl.multiple_of(F + k % TILES * FT, FT), FT)], s_du.at[b]),
         ]
 
+    def extra_in(c):
+        n = extra.shape[1]
+        return [
+            ld(hido.at[pl.ds(c * M, M), :], dyb.at[0, :, pl.ds(c * F, F)], s_dy.at[c]),
+            ld(dy.at[pl.ds(c * M, M), pl.ds(0, n)], dyb.at[1, :, pl.ds(c * n, n)], s_fd.at[c]),
+        ]
+
+    def extra_out(u):
+        rows, cols = pl.ds(pl.multiple_of(u % 2 * (F // 2), F // 2), F // 2), pl.ds(pl.multiple_of(u // 2 * FT, FT), FT)
+        return ld(fout.at[u % 2], extra.at[rows, cols], s_fo.at[u % 2])
+
     def fin(e, c):
         return ld(rsend.at[e, 2], piece.at[pl.ds(pl.multiple_of(c * M + e * H, H), H), :], s_fin.at[e])
 
@@ -142,6 +154,16 @@
         rows = pl.ds(e * H, H)
         total = own[g % 2, rows] + precv[(g + 4) % 4, rows].astype(F32) + rrecv[e, src].astype(F32)
         rsend[e, dst] = total.astype(BF)
+
+    def extra_piece(u):
+        n, half = extra.shape[1], F // 2
+        total = None
+        for c in range(CHUNKS):
+            h = dyb[0, :, pl.ds(pl.multiple_of(c * F + u % 2 * half, half), half)]
+            d = dyb[1, :, pl.ds(pl.multiple_of(c * n + u // 2 * FT, FT), FT)]
+            term = tn(h, d)
+            total = term if c == 0 else total + term
+        fout[u % 2] = total.astype(BF)
 
     def dh_ready(k):
         wait(dh_in(k))
@@ -283,6 +305,22 @@
             dg[...] = dgn[...]
             du[...] = dun[...]
 
+        @pl.when(t == 8 * (CHUNKS - 1))
+        def _():
+            for b in range(CHUNKS):
+                wait(extra_in(b))
+
+        @pl.when(t > 8 * (CHUNKS - 1))
+        def _():
+            u = t - 8 * (CHUNKS - 1) - 1
+
+            @pl.when(u >= 2)
+            def _():
+                extra_out(u - 2).wait()
+
+            extra_piece(u)
+            extra_out(u).start()
+
         @pl.when(ends)
         def _():
             for e in range(2):
@@ -316,11 +354,22 @@
         @pl.when(t + 3 < STEPS)
         def _():
             start(par_w(t + 3))
+
+        @pl.when(t == 8 * (CHUNKS - 1) - 1)
+        def _():
+            for k in (CHUNKS * TILES - 2, CHUNKS * TILES - 1):
+                wait(dh_out(k, dgn, dun))
+            for b in range(CHUNKS):
+                start(extra_in(b))
 
     part(STEPS - 1).wait_recv()
     part(STEPS - 1).wait_send()
     for e in range(2):
         fin(e, CHUNKS - 2).wait()
+        if e == 1:
+            extra_out(EXTRA - 3).wait()
+            extra_piece(EXTRA - 1)
+            extra_out(EXTRA - 1).start()
         ring(e, SENDS - 1).wait_recv()
         add(e, STEPS - 1, (SENDS - 1) % 3, 2)
         fin(e, CHUNKS - 1).start()
@@ -328,8 +377,8 @@
         ring(e, SENDS - 2).wait_send()
         ring(e, SENDS - 1).wait_send()
         fin(e, CHUNKS - 1).wait()
-    wait(dh_out(CHUNKS * TILES - 2, dgn, dun))
-    wait(dh_out(CHUNKS * TILES - 1, dgn, dun))
+    extra_out(EXTRA - 2).wait()
+    extra_out(EXTRA - 1).wait()
 
 
 def reduce_call(dy, wd, gate, up, wg, wu):
@@ -342,13 +391,13 @@
     return pl.pallas_call(
         reduce_kernel,
         in_specs=[hbm] * 6,
-        out_specs=[hbm] * 3,
-        out_shape=[jax.ShapeDtypeStruct((T, n), BF) for n in (2 * F, F, W)],
+        out_specs=[hbm] * 4,
+        out_shape=[jax.ShapeDtypeStruct(n, BF) for n in ((T, 2 * F), (T, F), (T, W), (F, EXTRA // 2 * FT))],
         scratch_shapes=[
             v((2, M, D), BF), v((2, FT, D), BF), v((2, M, FT), BF), v((2, M, FT), BF),
             v((M, F), BF), v((M, F), BF), v((M, F), BF), v((M, F), BF), v((2, M, FT), BF), v((2, 2 * W, F), BF), v((2, 2 * W, F), BF),
-            v((2, M, W), F32), v((4, M, W), BF), v((2, M, W), BF), v((2, 4, M // 2, W), BF), v((2, 3, M // 2, W), BF),
-            dma((4,)), *[dma((2,))] * 11,
+            v((2, M, W), F32), v((4, M, W), BF), v((2, M, W), BF), v((2, 4, M // 2, W), BF), v((2, 3, M // 2, W), BF), v((2, F // 2, FT), BF),
+            dma((4,)), dma((4,)), dma((2,)), *[dma((2,))] * 11,
             dma((2,)), dma((4,)), dma((2, 2)), dma((2, 3)), reg((2,)), reg,
         ],
         compiler_params=pltpu.CompilerParams(collective_id=0, has_side_effects=True, vmem_limit_bytes=VMEM_LIMIT),
@@ -356,35 +405,41 @@
     )(dy, wd, gate, up, wg, wu)
 
 
-def gate_up_grads(x, dgu, bm):
+ANY = pl.BlockSpec(memory_space=pl.ANY)
+RESIDENT = pl.BlockSpec(memory_space=pltpu.VMEM)
+
+
+def gate_up_grads(x, dgu, extra, dw_down, bm):
     T, D = x.shape
     F = dgu.shape[1] // 2
-
-    def body(x_ref, d_ref, og, ou):
+    steps = D // bm
+    n = extra.shape[1]
+
+    def body(x_ref, d_ref, e_ref, w_ref, og, ou, ow):
+        ow[...] = e_ref[...]
         both = tn(x_ref[...], d_ref[...])
         og[...] = both[:, :F].astype(BF)
         ou[...] = both[:, F:].astype(BF)
 
+    some = pl.BlockSpec((F // steps, n), lambda i: (i, 0))
+    extra = pltpu.with_memory_space_constraint(extra, pltpu.HBM)
     return pl.pallas_call(
         body,
-        grid=(D // bm,),
-        in_specs=[
-            pl.BlockSpec((T, bm), lambda i: (0, i)),
-            pl.BlockSpec((T, 2 * F), lambda i: (0, 0), pipeline_mode=pl.Buffered(1)),
-        ],
-        out_specs=[pl.BlockSpec((bm, F), lambda i: (i, 0))] * 2,
-        out_shape=[jax.ShapeDtypeStruct((D, F), BF)] * 2,
-        compiler_params=pltpu.CompilerParams(vmem_limit_bytes=VMEM_LIMIT),
+        grid=(steps,),
+        in_specs=[pl.BlockSpec((T, bm), lambda i: (0, i)), RESIDENT, some, ANY],
+        out_specs=[pl.BlockSpec((bm, F), lambda i: (i, 0))] * 2 + [some],
+        out_shape=[jax.ShapeDtypeStruct((D, F), BF)] * 2 + [jax.ShapeDtypeStruct((F, D), BF)],
+        input_output_aliases={3: 2},
+        compiler_params=pltpu.CompilerParams(vmem_limit_bytes=26 * 2**20),
         cost_estimate=pl.CostEstimate(flops=4 * T * D * F, bytes_accessed=2 * (T * D + 2 * T * F + 2 * D * F), transcendentals=0),
         name="dw_gate_up",
-    )(x, dgu)
+    )(x, dgu, extra, dw_down)
 
 
 def down_grad(hid, dy, bn, lo, hi, moved=(), prev=()):
     T, D = dy.shape
     F = hid.shape[1]
     steps = hi - lo
-    mb = T // steps
 
     def body(h_ref, dy_ref, *refs):
         if moved:
@@ -392,20 +447,17 @@
         o_ref = refs[-2] if moved else refs[-1]
         o_ref[...] = tn(h_ref[...], dy_ref[...]).astype(BF)
 
+    mb = T // steps
+    whole = pl.BlockSpec((T, F), lambda i: (0, 0), pipeline_mode=pl.Buffered(1)) if moved else RESIDENT
     rows = [pl.BlockSpec((mb, D), lambda i: (i, 0))] if moved else []
     return pl.pallas_call(
         body,
         grid=(steps,),
-        in_specs=[
-            pl.BlockSpec((T, F), lambda i: (0, 0), pipeline_mode=pl.Buffered(1)),
-            pl.BlockSpec((T, bn), lambda i: (0, lo + i)),
-            *rows,
-            *[pl.BlockSpec(memory_space=pl.ANY)] * len(prev),
-        ],
+        in_specs=[whole, pl.BlockSpec((T, bn), lambda i: (0, lo + i)), *rows, *[ANY] * len(prev)],
         out_specs=[pl.BlockSpec((F, bn), lambda i: (0, lo + i)), *rows],
         out_shape=[jax.ShapeDtypeStruct((F, D), BF), *[jax.ShapeDtypeStruct((T, D), BF)] * len(moved)],
         input_output_aliases={2 + len(moved): 0} if prev else {},
-        compiler_params=pltpu.CompilerParams(vmem_limit_bytes=VMEM_LIMIT),
+        compiler_params=pltpu.CompilerParams(vmem_limit_bytes=(36 if moved else 20) * 2**20),
         cost_estimate=pl.CostEstimate(
             flops=2 * T * F * bn * steps,
             bytes_accessed=2 * (T * F + (T + F) * bn * steps + 2 * T * D * len(moved)),
@@ -418,12 +470,12 @@
 def solution(mesh):
     def step(x, dy, gate, up, w_gate, w_up, w_down):
         D = x.shape[1]
-        dgu, hid, piece = reduce_call(dy, w_down, gate, up, w_gate, w_up)
+        dgu, hid, piece, extra = reduce_call(dy, w_down, gate, up, w_gate, w_up)
         gathered = lax.all_gather(piece, "tp", axis=1, tiled=True)
-        dw_gate, dw_up = gate_up_grads(x, dgu, D // 16)
         bn = D // 16
-        first = down_grad(hid, dy, bn, 0, 8)
-        dw_down, dx = down_grad(hid, dy, bn, 8, 16, (gathered,), first)
+        (dw_down,) = down_grad(hid, dy, bn, extra.shape[1] // bn, 12)
+        dw_gate, dw_up, dw_down = gate_up_grads(x, dgu, extra, dw_down, D // 16)
+        dw_down, dx = down_grad(hid, dy, bn // 2, 24, 32, (gathered,), (dw_down,))
         return dx, dw_gate, dw_up, dw_down
 
     tokens, columns, rows = P("dp", None), P(None, "tp"), P("tp", None)

time: 465 us -> 467 us (level)
  local copies, waits for them, and re-layouts: 0 us -> 6.16 us
    unnamed x0 -> x6, local copies, waits for them, and re-layouts: none -> 6.16 us
  transfers between devices with their start and end apart: 1 -> 1, of which waited for: 0 -> 0; matrix products, arithmetic and copies ran while one was open for 0% -> 0% of each run, Pallas kernels for 36% -> 37%
where the time goes in v3:
time: 467 us
  Pallas kernels  447 us (96%)
  between operations  14 us (3%)
  local copies, waits for them, and re-layouts  6.16 us (1%)
    pallas_call x1, Pallas kernels, reduce_call(): pl.pallas_call(reduce_kernel, in_specs=[hbm] * 6, out_specs=[hbm] * 4, ou...  242 us
    pallas_call x1, Pallas kernels, gate_up_grads(): pl.pallas_call(body, grid=(steps,), in_specs=[pl.BlockSpec((T, bm), lambd...  127 us
    pallas_call x2, Pallas kernels, down_grad(): pl.pallas_call(body, grid=(steps,), in_specs=[whole, pl.BlockSpec((T, bn)...  77.7 us
  transfers between devices with their start and end apart: 1, of which 0 were waited for; matrix products, arithmetic and copies ran while one was open for 0% of the time, Pallas kernels for 37%

profile of v3, /device:TPU:0, one launch (start us, length us, event | category | flops | bytes accessed | tf_op | source)
XLA Modules:
  0.0 466.9 jit_solution(2208093291295198161)
XLA Ops:
  7.2 0.0 all-gather.2.cloned.1.call-start
  7.2 241.6 %dx_reduce.1 = (bf16[2048,3584]{1,0:T(8,128)(2,1)}, bf16[2048,1792]{1,0:T(8,128)(2,1)}, bf16[2048,512]{1,0:T(8,128)(2,1)}, bf16[1792,1024]{1,0:T(8,128)(2,1)}) custom-call(bf16[2048,8192]{1,0:T(8,128)(2,1)} %dy_ref.3, bf16[1792,8192]{1,0:T(8,128)(2,1)} %wd.1, bf16[2048,1792]{1,0:T(8,128)(2,1)} %gate.1, bf16[2048,1792]{1,0:T(8,128)(2,1)} %up.1, ...), custom_call_target="tpu_custom_call" | custom-call | tf_op jit(solution)/shard_map/dx_reduce/pallas_call | solution.py:391
  248.8 0.0 all-gather.2.cloned.1.call-update
  248.8 0.0 copy-start
  248.8 3.1 copy-done
  251.9 0.0 copy-start.2
  251.9 43.2 %dw_down.2.w_ref = bf16[1792,8192]{1,0:T(8,128)(2,1)} custom-call(bf16[2048,1792]{1,0:T(8,128)(2,1)S(1)} %copy-done, bf16[2048,8192]{1,0:T(8,128)(2,1)} %dy_ref.3), custom_call_target="tpu_custom_call" | custom-call | flops 37580963840 | bytes 46661632 | tf_op jit(solution)/shard_map/dw_down/pallas_call | solution.py:453
  295.1 0.0 copy-done.2
  295.1 127.4 %dw_gate_up.1 = (bf16[8192,1792]{1,0:T(8,128)(2,1)}, bf16[8192,1792]{1,0:T(8,128)(2,1)}, bf16[1792,8192]{1,0:T(8,128)(2,1)}) custom-call(bf16[2048,8192]{1,0:T(8,128)(2,1)} %x_ref.1, bf16[2048,3584]{1,0:T(8,128)(2,1)S(1)} %copy-done.2, bf16[1792,1024]{1,0:T(8,128)(2,1)} %get-tuple-element.16.e_ref, ...), custom_call_target="tpu_custom_call", output_to_operand_aliasing={{2}: (3, {})} | custom-call | flops 120259084288 | bytes 106954752 | tf_op jit(solution)/shard_map/dw_gate_up/pallas_call | solution.py:426
  422.5 0.0 all-gather.2.cloned.1.call-done.refs_0_
  422.5 0.0 copy-start.1
  422.5 3.1 copy-done.1
  425.6 34.5 %dw_down.3 = (bf16[1792,8192]{1,0:T(8,128)(2,1)}, bf16[2048,8192]{1,0:T(8,128)(2,1)}) custom-call(bf16[2048,1792]{1,0:T(8,128)(2,1)S(1)} %copy-done.1, bf16[2048,8192]{1,0:T(8,128)(2,1)} %dy_ref.3, bf16[2048,8192]{1,0:T(8,128)(2,1)} %all-gather.2.cloned.1.call-done.refs_0_, bf16[1792,8192]{1,0:T(8,128)(2,1)} %get-tuple-element.17.refs_1_), custom_call_target="tpu_custom_call", output_to_operand_aliasing={{0}: (3, {})} | custom-call | flops 15032385536 | bytes 90177536 | tf_op jit(solution)/shard_map/dw_down/pallas_call | solution.py:453
Async XLA Ops:
  7.2 415.3 %all-gather.2.cloned.1.call-start = ((), (), s32[]{:S(2)}) async-start(), calls=%async_computation | async-start | bytes 35651584 | tf_op jit(solution)/shard_map/all_gather | solution.py:474
  248.8 3.1 copy-start
  251.9 43.2 %copy-start.2 = (bf16[2048,3584]{1,0:T(8,128)(2,1)S(1)}, bf16[2048,3584]{1,0:T(8,128)(2,1)}, u32[]{:S(2)}) copy-start(bf16[2048,3584]{1,0:T(8,128)(2,1)} %get-tuple-element.15.d_ref) | copy-start | bytes 44040196
  422.5 3.1 copy-start.1
Sparse Core Ops, SparseCore 0:
  248.9 166.6 all-gather.1

commit v4 on v3

--- a/solution.py
+++ b/solution.py
@@ -1,3 +1,5 @@
+import functools
+
 import jax
 import jax.numpy as jnp
 from jax import lax
@@ -297,7 +299,18 @@
 
         @pl.when((s < 7) & (c == CHUNKS - 1))
         def _():
+            @pl.when(s == 0)
+            def _():
+                for b in range(CHUNKS):
+                    wait(extra_in(b))
+
+            @pl.when(s >= 2)
+            def _():
+                extra_out(s - 2).wait()
+
             par_tile(t + 1, dg, du)
+            extra_piece(s)
+            extra_out(s).start()
 
         @pl.when((s == 7) & (c < CHUNKS - 1))
         def _():
@@ -305,22 +318,6 @@
             dg[...] = dgn[...]
             du[...] = dun[...]
 
-        @pl.when(t == 8 * (CHUNKS - 1))
-        def _():
-            for b in range(CHUNKS):
-                wait(extra_in(b))
-
-        @pl.when(t > 8 * (CHUNKS - 1))
-        def _():
-            u = t - 8 * (CHUNKS - 1) - 1
-
-            @pl.when(u >= 2)
-            def _():
-                extra_out(u - 2).wait()
-
-            extra_piece(u)
-            extra_out(u).start()
-
         @pl.when(ends)
         def _():
             for e in range(2):
@@ -355,12 +352,21 @@
         def _():
             start(par_w(t + 3))
 
+        @pl.when(t == 8 * (CHUNKS - 2) + 2)
+        def _():
+            for b in range(CHUNKS - 1):
+                extra_in(b)[0].start()
+
+        @pl.when(t == 8 * (CHUNKS - 1) - 2)
+        def _():
+            for b in range(CHUNKS):
+                extra_in(b)[1].start()
+
         @pl.when(t == 8 * (CHUNKS - 1) - 1)
         def _():
             for k in (CHUNKS * TILES - 2, CHUNKS * TILES - 1):
                 wait(dh_out(k, dgn, dun))
-            for b in range(CHUNKS):
-                start(extra_in(b))
+            extra_in(CHUNKS - 1)[0].start()
 
     part(STEPS - 1).wait_recv()
     part(STEPS - 1).wait_send()
@@ -436,28 +442,125 @@
     )(x, dgu, extra, dw_down)
 
 
+def down_kernel(lo, steps, moving, *refs):
+    if moving:
+        hid, dy, src, _, out, dst, hidb, dyb, ob, cb, s_h, s_d, s_o, s_in, s_out = refs
+    else:
+        hid, dy, out, hidb, dyb, ob, acc, s_h, s_d, s_o = refs
+    ld = pltpu.make_async_copy
+    T = hid.shape[0]
+    bn = dyb.shape[2]
+    half = T // 2
+
+    def cols(i):
+        return pl.ds(pl.multiple_of((lo + i) * bn, bn), bn)
+
+    def h_in(p):
+        rows = pl.ds(p * half, half)
+        return ld(hid.at[rows, :], hidb.at[rows, :], s_h.at[p])
+
+    def dy_in(i, p):
+        rows = pl.ds(p * half, half)
+        return ld(dy.at[rows, cols(i)], dyb.at[i % 2, rows], s_d.at[i % 2, p])
+
+    def put(i):
+        return ld(ob.at[i % 2], out.at[:, cols(i)], s_o.at[i % 2])
+
+    if moving:
+        n = cb.shape[1]
+
+        def rows_at(k):
+            return pl.ds(pl.multiple_of(k * n, n), n)
+
+        def come(k):
+            return ld(src.at[rows_at(k), :], cb.at[k % 8], s_in.at[k % 8])
+
+        def go(k):
+            return ld(cb.at[k % 8], dst.at[rows_at(k), :], s_out.at[k % 8])
+
+    for p in range(2):
+        h_in(p).start()
+        dy_in(0, p).start()
+    if moving:
+        for k in range(4):
+            come(k).start()
+    for p in range(2):
+        dy_in(1, p).start()
+
+    def block(i):
+        for p in range(2):
+            dy_in(i, p).wait()
+
+        @pl.when(i >= 2)
+        def _():
+            put(i - 2).wait()
+
+        if moving:
+            for e in range(2):
+                come(2 * i + e).wait()
+                go(2 * i + e).start()
+
+            @pl.when(i >= 2)
+            def _():
+                for e in range(2):
+                    go(2 * i - 4 + e).wait()
+
+            @pl.when(i + 2 < steps)
+            def _():
+                for e in range(2):
+                    come(2 * i + 4 + e).start()
+
+        ob[i % 2] = tn(hidb[...], dyb[i % 2]).astype(BF)
+        end(i)
+
+    def end(i):
+        put(i).start()
+
+        @pl.when(i + 2 < steps)
+        def _():
+            for p in range(2):
+                dy_in(i + 2, p).start()
+
+    if moving:
+        for p in range(2):
+            h_in(p).wait()
+        pl.loop(0, steps)(block)
+        for k in range(2 * steps - 4, 2 * steps):
+            go(k).wait()
+    else:
+        for p in range(2):
+            h_in(p).wait()
+            dy_in(0, p).wait()
+            rows = pl.ds(p * half, half)
+            term = tn(hidb[rows], dyb[0, rows])
+            if p == 0:
+                acc[...] = term
+            else:
+                ob[0] = (acc[...] + term).astype(BF)
+        end(0)
+        pl.loop(1, steps)(block)
+    put(steps - 2).wait()
+    put(steps - 1).wait()
+
+
 def down_grad(hid, dy, bn, lo, hi, moved=(), prev=()):
     T, D = dy.shape
     F = hid.shape[1]
     steps = hi - lo
-
-    def body(h_ref, dy_ref, *refs):
-        if moved:
-            refs[-1][...] = refs[0][...]
-        o_ref = refs[-2] if moved else refs[-1]
-        o_ref[...] = tn(h_ref[...], dy_ref[...]).astype(BF)
-
-    mb = T // steps
-    whole = pl.BlockSpec((T, F), lambda i: (0, 0), pipeline_mode=pl.Buffered(1)) if moved else RESIDENT
-    rows = [pl.BlockSpec((mb, D), lambda i: (i, 0))] if moved else []
+    hbm = pl.BlockSpec(memory_space=pltpu.HBM)
+    dma, v = pltpu.SemaphoreType.DMA, pltpu.VMEM
+    hid, dy = (pltpu.with_memory_space_constraint(a, pltpu.HBM) for a in (hid, dy))
+    scratch = [v((T, F), BF), v((2, T, bn), BF), v((2, F, bn), BF)]
+    scratch.append(v((8, T // (2 * steps), D), BF) if moved else v((F, bn), F32))
+    scratch += [dma((2,)), dma((2, 2)), dma((2,))] + [dma((8,))] * (2 * len(moved))
     return pl.pallas_call(
-        body,
-        grid=(steps,),
-        in_specs=[whole, pl.BlockSpec((T, bn), lambda i: (0, lo + i)), *rows, *[ANY] * len(prev)],
-        out_specs=[pl.BlockSpec((F, bn), lambda i: (0, lo + i)), *rows],
+        functools.partial(down_kernel, lo, steps, bool(moved)),
+        in_specs=[hbm] * (2 + len(moved) + len(prev)),
+        out_specs=[hbm] * (1 + len(moved)),
         out_shape=[jax.ShapeDtypeStruct((F, D), BF), *[jax.ShapeDtypeStruct((T, D), BF)] * len(moved)],
+        scratch_shapes=scratch,
         input_output_aliases={2 + len(moved): 0} if prev else {},
-        compiler_params=pltpu.CompilerParams(vmem_limit_bytes=(36 if moved else 20) * 2**20),
+        compiler_params=pltpu.CompilerParams(vmem_limit_bytes=(48 if moved else 30) * 2**20),
         cost_estimate=pl.CostEstimate(
             flops=2 * T * F * bn * steps,
             bytes_accessed=2 * (T * F + (T + F) * bn * steps + 2 * T * D * len(moved)),

time: 467 us -> 458 us (0.981)
  local copies, waits for them, and re-layouts: 6.16 us -> 0.02 us
    unnamed x6 -> x8, local copies, waits for them, and re-layouts: 6.16 us -> 0.02 us
  transfers between devices with their start and end apart: 1 -> 1, of which waited for: 0 -> 0; matrix products, arithmetic and copies ran while one was open for 0% -> 0% of each run, Pallas kernels for 37% -> 38%
where the time goes in v4:
time: 458 us
  Pallas kernels  444 us (97%)
  between operations  14.1 us (3%)
    pallas_call x1, Pallas kernels, reduce_call(): pl.pallas_call(reduce_kernel, in_specs=[hbm] * 6, out_specs=[hbm] * 4, ou...  240 us
    pallas_call x1, Pallas kernels, gate_up_grads(): pl.pallas_call(body, grid=(steps,), in_specs=[pl.BlockSpec((T, bm), lambd...  128 us
    pallas_call x2, Pallas kernels, down_grad(): pl.pallas_call(functools.partial(down_kernel, lo, steps, bool(moved)), in...  75.5 us
  transfers between devices with their start and end apart: 1, of which 0 were waited for; matrix products, arithmetic and copies ran while one was open for 0% of the time, Pallas kernels for 38%

profile of v4, /device:TPU:0, one launch (start us, length us, event | category | flops | bytes accessed | tf_op | source)
XLA Modules:
  0.0 457.9 jit_solution(3801485998242688095)
XLA Ops:
  7.2 0.0 all-gather.2.cloned.1.call-start
  7.2 240.5 %dx_reduce.1 = (bf16[2048,3584]{1,0:T(8,128)(2,1)}, bf16[2048,1792]{1,0:T(8,128)(2,1)}, bf16[2048,512]{1,0:T(8,128)(2,1)}, bf16[1792,1024]{1,0:T(8,128)(2,1)}) custom-call(bf16[2048,8192]{1,0:T(8,128)(2,1)} %refs_1_.3, bf16[1792,8192]{1,0:T(8,128)(2,1)} %wd.1, bf16[2048,1792]{1,0:T(8,128)(2,1)} %gate.1, bf16[2048,1792]{1,0:T(8,128)(2,1)} %up.1, ...), custom_call_target="tpu_custom_call" | custom-call | tf_op jit(solution)/shard_map/dx_reduce/pallas_call | solution.py:397
  247.7 0.0 slice-start
  247.7 0.0 all-gather.2.cloned.1.call-update
  247.7 0.0 slice-start.1
  247.8 0.0 slice-start.2
  247.8 0.0 slice-start.3
  247.8 44.4 %dw_down.2.w_ref = bf16[1792,8192]{1,0:T(8,128)(2,1)} custom-call(bf16[2048,1792]{1,0:T(8,128)(2,1)} %get-tuple-element.13.refs_0_, bf16[2048,8192]{1,0:T(8,128)(2,1)} %refs_1_.3), custom_call_target="tpu_custom_call" | custom-call | flops 37580963840 | bytes 46661632 | tf_op jit(solution)/shard_map/dw_down/pallas_call | solution.py:556
  292.2 0.0 slice-done
  292.2 0.0 slice-done.1
  292.2 0.0 slice-done.2
  292.3 0.0 slice-done.3
  292.3 127.7 %dw_gate_up.1 = (bf16[8192,1792]{1,0:T(8,128)(2,1)}, bf16[8192,1792]{1,0:T(8,128)(2,1)}, bf16[1792,8192]{1,0:T(8,128)(2,1)}) custom-call(bf16[2048,8192]{1,0:T(8,128)(2,1)} %x_ref.1, bf16[2048,3584]{1,0:T(8,128)(2,1)S(1)} %bitcast.1, bf16[1792,1024]{1,0:T(8,128)(2,1)} %get-tuple-element.16.e_ref, ...), custom_call_target="tpu_custom_call", output_to_operand_aliasing={{2}: (3, {})} | custom-call | flops 120259084288 | bytes 106954752 | tf_op jit(solution)/shard_map/dw_gate_up/pallas_call | solution.py:432
  420.0 0.0 all-gather.2.cloned.1.call-done.refs_2_
  420.0 31.1 %dw_down.3 = (bf16[1792,8192]{1,0:T(8,128)(2,1)}, bf16[2048,8192]{1,0:T(8,128)(2,1)}) custom-call(bf16[2048,1792]{1,0:T(8,128)(2,1)} %get-tuple-element.13.refs_0_, bf16[2048,8192]{1,0:T(8,128)(2,1)} %refs_1_.3, bf16[2048,8192]{1,0:T(8,128)(2,1)} %all-gather.2.cloned.1.call-done.refs_2_, ...), custom_call_target="tpu_custom_call", output_to_operand_aliasing={{0}: (3, {})} | custom-call | flops 15032385536 | bytes 90177536 | tf_op jit(solution)/shard_map/dw_down/pallas_call | solution.py:556
  (1 shorter events, 0.0 us)
Async XLA Ops:
  7.2 412.8 %all-gather.2.cloned.1.call-start = ((), (), s32[]{:S(2)}) async-start(), calls=%async_computation | async-start | bytes 35651584 | tf_op jit(solution)/shard_map/all_gather | solution.py:577
  247.7 44.5 %slice-start = ((s8[14680064]{0:T(1024)(128)(4,1)}), s8[2097152]{0:T(1024)(128)(4,1)S(1)}, s32[]{:S(2)}) async-start(s8[14680064]{0:T(1024)(128)(4,1)} %bitcast), calls=%async_computation.1 | async-start | bytes 4194304
  247.7 44.5 %slice-start.1 = ((s8[14680064]{0:T(1024)(128)(4,1)}), s8[4194304]{0:T(1024)(128)(4,1)S(1)}, s32[]{:S(2)}) async-start(s8[14680064]{0:T(1024)(128)(4,1)} %bitcast), calls=%async_computation.2 | async-start | bytes 8388608
  247.8 44.5 %slice-start.2 = ((s8[14680064]{0:T(1024)(128)(4,1)}), s8[4194304]{0:T(1024)(128)(4,1)S(1)}, s32[]{:S(2)}) async-start(s8[14680064]{0:T(1024)(128)(4,1)} %bitcast), calls=%async_computation.3 | async-start | bytes 8388608
  247.8 44.5 %slice-start.3 = ((s8[14680064]{0:T(1024)(128)(4,1)}), s8[4194304]{0:T(1024)(128)(4,1)S(1)}, s32[]{:S(2)}) async-start(s8[14680064]{0:T(1024)(128)(4,1)} %bitcast), calls=%async_computation.4 | async-start | bytes 8388608
Sparse Core Ops, SparseCore 0:
  247.9 167.3 all-gather.1

commit v5 on v4

--- a/solution.py
+++ b/solution.py
@@ -15,7 +15,7 @@
 TILES = 7
 STEPS = CHUNKS * CHIPS
 SENDS = CHUNKS * (CHIPS - 1)
-EXTRA = 8
+EXTRA = 12
 
 
 def nt(a, b):
@@ -146,15 +146,15 @@
 
     def own_tile(g):
         b, half = g % 2, pl.ds(0, W)
-        own[g % 2] = nt(dg[...], wgb[b, half]) + nt(du[...], wub[b, half])
+        term = nt(dg[...], wgb[b, half]) + nt(du[...], wub[b, half])
+        own[g % 2] = term + precv[g % 4].astype(F32)
 
     def par_tile(g, dg, du):
         b, half = (g + 1) % 2, pl.ds(W, W)
         psend[g % 2] = (nt(dg[...], wgb[b, half]) + nt(du[...], wub[b, half])).astype(BF)
 
     def add(e, g, src, dst):
-        rows = pl.ds(e * H, H)
-        total = own[g % 2, rows] + precv[(g + 4) % 4, rows].astype(F32) + rrecv[e, src].astype(F32)
+        total = own[g % 2, pl.ds(e * H, H)] + rrecv[e, src].astype(F32)
         rsend[e, dst] = total.astype(BF)
 
     def extra_piece(u):
@@ -167,11 +167,11 @@
             total = term if c == 0 else total + term
         fout[u % 2] = total.astype(BF)
 
-    def dh_ready(k):
+    def dh_ready(k, early=False):
         wait(dh_in(k))
-
-        @pl.when(k >= 2)
-        def _():
+        if early:
+            pl.when(k >= 2)(lambda: wait(dh_out(k - 2, dg, du)))
+        else:
             wait(dh_out(k - 2, dg, du))
 
     def dh_done(k, dg, du):
@@ -202,7 +202,7 @@
             for p in range(4):
                 dy_in(0, p).wait()
 
-        dh_ready(k)
+        dh_ready(k, early=True)
         dh_tile(k, dg, du)
         dh_done(k, dg, du)
 
@@ -233,40 +233,45 @@
         src = got * ((m + 2) % 3) + (1 - got) * 3
         dst = (1 - last) * (m % 2) + last * 2
 
-        wait(own_w(t))
-
-        @pl.when(t + 1 < STEPS)
-        def _():
-            wait(par_w(t + 1))
-
-        @pl.when((s == 0) & (c < CHUNKS - 1))
-        def _():
-            for p in range(4):
-                dy_in(c + 1, p).wait()
-
         @pl.when(has_dh)
         def _():
             dh_ready(k)
 
+        @pl.when(jnp.logical_not(has_dh))
+        def _():
+            wait(own_w(t))
+
+            @pl.when(t + 1 < STEPS)
+            def _():
+                wait(par_w(t + 1))
+
+        @pl.when(s == 0)
+        def _():
+            @pl.when(c < CHUNKS - 1)
+            def _():
+                for p in range(4):
+                    dy_in(c + 1, p).wait()
+
+            @pl.when(t >= 16)
+            def _():
+                for e in range(2):
+                    fin(e, c - 2).wait()
+
         @pl.when(adds)
         def _():
-            part(g).wait_recv()
             part(g).wait_send()
 
-        @pl.when(sends & (m >= 2))
-        def _():
-            for e in range(2):
-                ring(e, m - 2).wait_send()
-
-        @pl.when(sends & (m >= 3))
-        def _():
-            for e in range(2):
-                pl.semaphore_wait(c_ring.at[e], 1)
-
-        @pl.when(ends & (t >= 16))
-        def _():
-            for e in range(2):
-                fin(e, c - 2).wait()
+        @pl.when(sends)
+        def _():
+            @pl.when(m >= 2)
+            def _():
+                for e in range(2):
+                    ring(e, m - 2).wait_send()
+
+            @pl.when(m >= 3)
+            def _():
+                for e in range(2):
+                    pl.semaphore_wait(c_ring.at[e], 1)
 
         def pass_on(e):
             @pl.when(takes)
@@ -285,38 +290,55 @@
         def _():
             dh_tile(k, dgn, dun)
 
-        @pl.when(jnp.logical_not(has_dh))
-        def _():
-            own_tile(t)
+        @pl.when((s < 7) & (c == CHUNKS - 1))
+        def _():
+            @pl.when(s == 0)
+            def _():
+                for b in range(CHUNKS):
+                    wait(extra_in(b))
+
+            @pl.when(s >= 2)
+            def _():
+                extra_out(s - 2).wait()
+
+            par_tile(t + 1, dg, du)
+            extra_piece(s)
+            extra_out(s).start()
+
+        @pl.when((s == 7) & (c < CHUNKS - 1))
+        def _():
+            par_tile(t + 1, dgn, dun)
 
         pass_on(1)
 
         @pl.when(has_dh)
         def _():
+            wait(own_w(t))
+            wait(par_w(t + 1))
+            part(t).wait_recv()
             own_tile(t)
             par_tile(t + 1, dg, du)
             dh_done(k, dgn, dun)
-
-        @pl.when((s < 7) & (c == CHUNKS - 1))
-        def _():
-            @pl.when(s == 0)
-            def _():
-                for b in range(CHUNKS):
-                    wait(extra_in(b))
-
-            @pl.when(s >= 2)
-            def _():
-                extra_out(s - 2).wait()
-
-            par_tile(t + 1, dg, du)
-            extra_piece(s)
-            extra_out(s).start()
-
-        @pl.when((s == 7) & (c < CHUNKS - 1))
-        def _():
-            par_tile(t + 1, dgn, dun)
-            dg[...] = dgn[...]
-            du[...] = dun[...]
+            start(own_w(t + 2))
+            start(par_w(t + 3))
+
+        @pl.when(jnp.logical_not(has_dh))
+        def _():
+            part(t).wait_recv()
+            own_tile(t)
+
+            @pl.when((s == 7) & (c < CHUNKS - 1))
+            def _():
+                dg[...] = dgn[...]
+                du[...] = dun[...]
+
+            @pl.when(t + 2 < STEPS)
+            def _():
+                start(own_w(t + 2))
+
+            @pl.when(t + 3 < STEPS)
+            def _():
+                start(par_w(t + 3))
 
         @pl.when(ends)
         def _():
@@ -344,41 +366,40 @@
         def _():
             dy_in(c + 2, s).start()
 
-        @pl.when(t + 2 < STEPS)
-        def _():
-            start(own_w(t + 2))
-
-        @pl.when(t + 3 < STEPS)
-        def _():
-            start(par_w(t + 3))
-
-        @pl.when(t == 8 * (CHUNKS - 2) + 2)
-        def _():
-            for b in range(CHUNKS - 1):
-                extra_in(b)[0].start()
-
-        @pl.when(t == 8 * (CHUNKS - 1) - 2)
-        def _():
-            for b in range(CHUNKS):
-                extra_in(b)[1].start()
-
-        @pl.when(t == 8 * (CHUNKS - 1) - 1)
-        def _():
-            for k in (CHUNKS * TILES - 2, CHUNKS * TILES - 1):
-                wait(dh_out(k, dgn, dun))
-            extra_in(CHUNKS - 1)[0].start()
-
-    part(STEPS - 1).wait_recv()
+        @pl.when(c == CHUNKS - 2)
+        def _():
+            @pl.when(s == 2)
+            def _():
+                for b in range(CHUNKS - 1):
+                    extra_in(b)[0].start()
+
+            @pl.when(s == 6)
+            def _():
+                for b in range(CHUNKS):
+                    extra_in(b)[1].start()
+
+            @pl.when(s == 7)
+            def _():
+                for k in (CHUNKS * TILES - 2, CHUNKS * TILES - 1):
+                    wait(dh_out(k, dgn, dun))
+                extra_in(CHUNKS - 1)[0].start()
+
     part(STEPS - 1).wait_send()
-    for e in range(2):
-        fin(e, CHUNKS - 2).wait()
-        if e == 1:
-            extra_out(EXTRA - 3).wait()
-            extra_piece(EXTRA - 1)
-            extra_out(EXTRA - 1).start()
-        ring(e, SENDS - 1).wait_recv()
-        add(e, STEPS - 1, (SENDS - 1) % 3, 2)
-        fin(e, CHUNKS - 1).start()
+
+    @pl.loop(7, EXTRA)
+    def _(u):
+        extra_out(u - 2).wait()
+        extra_piece(u)
+        extra_out(u).start()
+
+        @pl.when(u >= EXTRA - 2)
+        def _():
+            e = u - (EXTRA - 2)
+            fin(e, CHUNKS - 2).wait()
+            ring(e, SENDS - 1).wait_recv()
+            add(e, STEPS - 1, (SENDS - 1) % 3, 2)
+            fin(e, CHUNKS - 1).start()
+
     for e in range(2):
         ring(e, SENDS - 2).wait_send()
         ring(e, SENDS - 1).wait_send()

time: 458 us -> 457 us (level)
  transfers between devices with their start and end apart: 1 -> 1, of which waited for: 0 -> 0; matrix products, arithmetic and copies ran while one was open for 0% -> 0% of each run, Pallas kernels for 38% -> 37%
where the time goes in v5:
time: 457 us
  Pallas kernels  442 us (97%)
  between operations  14.1 us (3%)
    pallas_call x1, Pallas kernels, reduce_call(): pl.pallas_call(reduce_kernel, in_specs=[hbm] * 6, out_specs=[hbm] * 4, ou...  243 us
    pallas_call x1, Pallas kernels, gate_up_grads(): pl.pallas_call(body, grid=(steps,), in_specs=[pl.BlockSpec((T, bm), lambd...  128 us
    pallas_call x2, Pallas kernels, down_grad(): pl.pallas_call(functools.partial(down_kernel, lo, steps, bool(moved)), in...  71.5 us
  transfers between devices with their start and end apart: 1, of which 0 were waited for; matrix products, arithmetic and copies ran while one was open for 0% of the time, Pallas kernels for 37%

profile of v5, /device:TPU:0, one launch (start us, length us, event | category | flops | bytes accessed | tf_op | source)
XLA Modules:
  0.0 456.6 jit_solution(9902016654708300972)
XLA Ops:
  7.2 0.0 all-gather.2.cloned.1.call-start
  7.2 243.3 %dx_reduce.1 = (bf16[2048,3584]{1,0:T(8,128)(2,1)}, bf16[2048,1792]{1,0:T(8,128)(2,1)}, bf16[2048,512]{1,0:T(8,128)(2,1)}, bf16[1792,1536]{1,0:T(8,128)(2,1)}) custom-call(bf16[2048,8192]{1,0:T(8,128)(2,1)} %refs_1_.3, bf16[1792,8192]{1,0:T(8,128)(2,1)} %wd.1, bf16[2048,1792]{1,0:T(8,128)(2,1)} %gate.1, bf16[2048,1792]{1,0:T(8,128)(2,1)} %up.1, ...), custom_call_target="tpu_custom_call" | custom-call | tf_op jit(solution)/shard_map/dx_reduce/pallas_call | solution.py:418
  250.6 0.0 slice-start
  250.6 0.0 all-gather.2.cloned.1.call-update
  250.6 0.0 slice-start.1
  250.6 0.0 slice-start.2
  250.6 0.0 slice-start.3
  250.6 40.4 %dw_down.2.w_ref = bf16[1792,8192]{1,0:T(8,128)(2,1)} custom-call(bf16[2048,1792]{1,0:T(8,128)(2,1)} %get-tuple-element.13.refs_0_, bf16[2048,8192]{1,0:T(8,128)(2,1)} %refs_1_.3), custom_call_target="tpu_custom_call" | custom-call | flops 33822867456 | bytes 42729472 | tf_op jit(solution)/shard_map/dw_down/pallas_call | solution.py:577
  291.1 0.0 slice-done
  291.1 0.0 slice-done.1
  291.1 0.0 slice-done.2
  291.1 0.0 slice-done.3
  291.1 127.5 %dw_gate_up.1 = (bf16[8192,1792]{1,0:T(8,128)(2,1)}, bf16[8192,1792]{1,0:T(8,128)(2,1)}, bf16[1792,8192]{1,0:T(8,128)(2,1)}) custom-call(bf16[2048,8192]{1,0:T(8,128)(2,1)} %x_ref.1, bf16[2048,3584]{1,0:T(8,128)(2,1)S(1)} %bitcast.1, bf16[1792,1536]{1,0:T(8,128)(2,1)} %get-tuple-element.16.e_ref, ...), custom_call_target="tpu_custom_call", output_to_operand_aliasing={{2}: (3, {})} | custom-call | flops 120259084288 | bytes 106954752 | tf_op jit(solution)/shard_map/dw_gate_up/pallas_call | solution.py:453
  418.6 0.0 all-gather.2.cloned.1.call-done.refs_2_
  418.6 31.1 %dw_down.3 = (bf16[1792,8192]{1,0:T(8,128)(2,1)}, bf16[2048,8192]{1,0:T(8,128)(2,1)}) custom-call(bf16[2048,1792]{1,0:T(8,128)(2,1)} %get-tuple-element.13.refs_0_, bf16[2048,8192]{1,0:T(8,128)(2,1)} %refs_1_.3, bf16[2048,8192]{1,0:T(8,128)(2,1)} %all-gather.2.cloned.1.call-done.refs_2_, ...), custom_call_target="tpu_custom_call", output_to_operand_aliasing={{0}: (3, {})} | custom-call | flops 15032385536 | bytes 90177536 | tf_op jit(solution)/shard_map/dw_down/pallas_call | solution.py:577
  (1 shorter events, 0.0 us)
Async XLA Ops:
  7.2 411.5 %all-gather.2.cloned.1.call-start = ((), (), s32[]{:S(2)}) async-start(), calls=%async_computation | async-start | bytes 35651584 | tf_op jit(solution)/shard_map/all_gather | solution.py:598
  250.6 40.5 %slice-start = ((s8[14680064]{0:T(1024)(128)(4,1)}), s8[2097152]{0:T(1024)(128)(4,1)S(1)}, s32[]{:S(2)}) async-start(s8[14680064]{0:T(1024)(128)(4,1)} %bitcast), calls=%async_computation.1 | async-start | bytes 4194304
  250.6 40.5 %slice-start.1 = ((s8[14680064]{0:T(1024)(128)(4,1)}), s8[4194304]{0:T(1024)(128)(4,1)S(1)}, s32[]{:S(2)}) async-start(s8[14680064]{0:T(1024)(128)(4,1)} %bitcast), calls=%async_computation.2 | async-start | bytes 8388608
  250.6 40.5 %slice-start.2 = ((s8[14680064]{0:T(1024)(128)(4,1)}), s8[4194304]{0:T(1024)(128)(4,1)S(1)}, s32[]{:S(2)}) async-start(s8[14680064]{0:T(1024)(128)(4,1)} %bitcast), calls=%async_computation.3 | async-start | bytes 8388608
  250.6 40.5 %slice-start.3 = ((s8[14680064]{0:T(1024)(128)(4,1)}), s8[4194304]{0:T(1024)(128)(4,1)S(1)}, s32[]{:S(2)}) async-start(s8[14680064]{0:T(1024)(128)(4,1)} %bitcast), calls=%async_computation.4 | async-start | bytes 8388608
Sparse Core Ops, SparseCore 0:
  250.7 165.9 all-gather.1

commit v6 on v5

--- a/solution.py
+++ b/solution.py
@@ -309,6 +309,12 @@
         def _():
             par_tile(t + 1, dgn, dun)
 
+        @pl.when(t == STEPS - 1)
+        def _():
+            extra_out(5).wait()
+            extra_piece(7)
+            extra_out(7).start()
+
         pass_on(1)
 
         @pl.when(has_dh)
@@ -386,20 +392,21 @@
 
     part(STEPS - 1).wait_send()
 
-    @pl.loop(7, EXTRA)
+    def end(e):
+        fin(e, CHUNKS - 2).wait()
+        ring(e, SENDS - 1).wait_recv()
+        add(e, STEPS - 1, (SENDS - 1) % 3, 2)
+        fin(e, CHUNKS - 1).start()
+
+    end(0)
+
+    @pl.loop(8, EXTRA)
     def _(u):
         extra_out(u - 2).wait()
         extra_piece(u)
         extra_out(u).start()
 
-        @pl.when(u >= EXTRA - 2)
-        def _():
-            e = u - (EXTRA - 2)
-            fin(e, CHUNKS - 2).wait()
-            ring(e, SENDS - 1).wait_recv()
-            add(e, STEPS - 1, (SENDS - 1) % 3, 2)
-            fin(e, CHUNKS - 1).start()
-
+    end(1)
     for e in range(2):
         ring(e, SENDS - 2).wait_send()
         ring(e, SENDS - 1).wait_send()

time: 457 us -> 456 us (level)
  no operation moved by 1% of the time
where the time goes in v6:
time: 456 us
  Pallas kernels  442 us (97%)
  between operations  14.1 us (3%)
    pallas_call x1, Pallas kernels, reduce_call(): pl.pallas_call(reduce_kernel, in_specs=[hbm] * 6, out_specs=[hbm] * 4, ou...  243 us
    pallas_call x1, Pallas kernels, gate_up_grads(): pl.pallas_call(body, grid=(steps,), in_specs=[pl.BlockSpec((T, bm), lambd...  128 us
    pallas_call x2, Pallas kernels, down_grad(): pl.pallas_call(functools.partial(down_kernel, lo, steps, bool(moved)), in...  71.5 us
  transfers between devices with their start and end apart: 1, of which 0 were waited for; matrix products, arithmetic and copies ran while one was open for 0% of the time, Pallas kernels for 37%

profile of v6, /device:TPU:0, one launch (start us, length us, event | category | flops | bytes accessed | tf_op | source)
XLA Modules:
  0.0 456.0 jit_solution(183720122635637920)
XLA Ops:
  7.2 0.0 all-gather.2.cloned.1.call-start
  7.2 242.7 %dx_reduce.1 = (bf16[2048,3584]{1,0:T(8,128)(2,1)}, bf16[2048,1792]{1,0:T(8,128)(2,1)}, bf16[2048,512]{1,0:T(8,128)(2,1)}, bf16[1792,1536]{1,0:T(8,128)(2,1)}) custom-call(bf16[2048,8192]{1,0:T(8,128)(2,1)} %refs_1_.3, bf16[1792,8192]{1,0:T(8,128)(2,1)} %wd.1, bf16[2048,1792]{1,0:T(8,128)(2,1)} %gate.1, bf16[2048,1792]{1,0:T(8,128)(2,1)} %up.1, ...), custom_call_target="tpu_custom_call" | custom-call | tf_op jit(solution)/shard_map/dx_reduce/pallas_call | solution.py:425
  250.0 0.0 slice-start
  250.0 0.0 all-gather.2.cloned.1.call-update
  250.0 0.0 slice-start.1
  250.0 0.0 slice-start.2
  250.0 0.0 slice-start.3
  250.0 40.4 %dw_down.2.w_ref = bf16[1792,8192]{1,0:T(8,128)(2,1)} custom-call(bf16[2048,1792]{1,0:T(8,128)(2,1)} %get-tuple-element.13.refs_0_, bf16[2048,8192]{1,0:T(8,128)(2,1)} %refs_1_.3), custom_call_target="tpu_custom_call" | custom-call | flops 33822867456 | bytes 42729472 | tf_op jit(solution)/shard_map/dw_down/pallas_call | solution.py:584
  290.4 0.0 slice-done
  290.5 0.0 slice-done.1
  290.5 0.0 slice-done.2
  290.5 0.0 slice-done.3
  290.5 127.5 %dw_gate_up.1 = (bf16[8192,1792]{1,0:T(8,128)(2,1)}, bf16[8192,1792]{1,0:T(8,128)(2,1)}, bf16[1792,8192]{1,0:T(8,128)(2,1)}) custom-call(bf16[2048,8192]{1,0:T(8,128)(2,1)} %x_ref.1, bf16[2048,3584]{1,0:T(8,128)(2,1)S(1)} %bitcast.1, bf16[1792,1536]{1,0:T(8,128)(2,1)} %get-tuple-element.16.e_ref, ...), custom_call_target="tpu_custom_call", output_to_operand_aliasing={{2}: (3, {})} | custom-call | flops 120259084288 | bytes 106954752 | tf_op jit(solution)/shard_map/dw_gate_up/pallas_call | solution.py:460
  418.0 0.0 all-gather.2.cloned.1.call-done.refs_2_
  418.0 31.1 %dw_down.3 = (bf16[1792,8192]{1,0:T(8,128)(2,1)}, bf16[2048,8192]{1,0:T(8,128)(2,1)}) custom-call(bf16[2048,1792]{1,0:T(8,128)(2,1)} %get-tuple-element.13.refs_0_, bf16[2048,8192]{1,0:T(8,128)(2,1)} %refs_1_.3, bf16[2048,8192]{1,0:T(8,128)(2,1)} %all-gather.2.cloned.1.call-done.refs_2_, ...), custom_call_target="tpu_custom_call", output_to_operand_aliasing={{0}: (3, {})} | custom-call | flops 15032385536 | bytes 90177536 | tf_op jit(solution)/shard_map/dw_down/pallas_call | solution.py:584
  (1 shorter events, 0.0 us)
Async XLA Ops:
  7.2 410.8 %all-gather.2.cloned.1.call-start = ((), (), s32[]{:S(2)}) async-start(), calls=%async_computation | async-start | bytes 35651584 | tf_op jit(solution)/shard_map/all_gather | solution.py:605
  250.0 40.5 %slice-start = ((s8[14680064]{0:T(1024)(128)(4,1)}), s8[2097152]{0:T(1024)(128)(4,1)S(1)}, s32[]{:S(2)}) async-start(s8[14680064]{0:T(1024)(128)(4,1)} %bitcast), calls=%async_computation.1 | async-start | bytes 4194304
  250.0 40.5 %slice-start.1 = ((s8[14680064]{0:T(1024)(128)(4,1)}), s8[4194304]{0:T(1024)(128)(4,1)S(1)}, s32[]{:S(2)}) async-start(s8[14680064]{0:T(1024)(128)(4,1)} %bitcast), calls=%async_computation.2 | async-start | bytes 8388608
  250.0 40.5 %slice-start.2 = ((s8[14680064]{0:T(1024)(128)(4,1)}), s8[4194304]{0:T(1024)(128)(4,1)S(1)}, s32[]{:S(2)}) async-start(s8[14680064]{0:T(1024)(128)(4,1)} %bitcast), calls=%async_computation.3 | async-start | bytes 8388608
  250.0 40.5 %slice-start.3 = ((s8[14680064]{0:T(1024)(128)(4,1)}), s8[4194304]{0:T(1024)(128)(4,1)S(1)}, s32[]{:S(2)}) async-start(s8[14680064]{0:T(1024)(128)(4,1)} %bitcast), calls=%async_computation.4 | async-start | bytes 8388608
Sparse Core Ops, SparseCore 0:
  250.1 165.9 all-gather.1
